TPU v7x, 32 devices: a whole 2x2x4 slice. The times are simulated.
32 devices in a mesh: blk: 8 (over z, core), section: 4 (over y, x).
Axes of the slice: x: 2, y: 2, z: 4, core: 2. Of those that a mesh axis runs over, the one named last changes fastest.
Arguments:
- hidden: bfloat16 [4, 2048, 4096], P('section', 'blk'), parts along dimension 1, may hold values from -6 to 6
- exit_layer: int32 [4096], P('blk'), parts along dimension 0, may hold values from 1 to 2
- lengths: int32 [4096], P('blk'), parts along dimension 0, may hold values from 1 to 16, as said below
- kv_cache: bfloat16 [4, 2048, 16, 256], P('section', 'blk'), parts along dimension 1, may hold values from -256 to 256
- norm_gain: bfloat16 [4, 4096], P('section'), may hold values from 0.5 to 1.5
- w_qkv: bfloat16 [4, 4096, 1280], P('section'), may hold values from -0.0625 to 0.0625
- w_out: bfloat16 [4, 1024, 4096], P('section'), may hold values from -0.1875 to 0.1875
Outputs:
- settled: bfloat16 [4096, 8192], P('blk', 'section'), parts along dimension 0
There are 8 independent parts, one for each index of `blk`. A program takes and returns all parts, laid end to end along the dimension named above; an argument that names none is the same for every part. Nothing has to cross between parts.
Inputs may be any that keep to these rules, and one draw needn't show every extreme that they name: `lengths`: some token has length 16.
All inputs are finite; a program needn't handle non-finite values.
Results may differ from a plain program's by a relative error of at most 0.03.
Values may be sent and summed in bfloat16 or wider, within the bound.
A program may use at most 64 MiB of HBM per device.

v0:
```python
import math

import jax
import jax.numpy as jnp
from jax import lax
from jax.sharding import PartitionSpec as P

BLOCK = 64
MICRO = 8


EPSILON = 1e-05
NEGATIVE = -1e30


def partner(value, axis, distance):
    return lax.ppermute(value, axis, [(i, i ^ 1 << distance) for i in range(lax.axis_size(axis))])


def shifted(value, axis, steps):
    count = lax.axis_size(axis)
    pairs = [(source, (source + steps) % count) for source in range(count)]
    return lax.ppermute(value, axis, pairs)


def body(hidden, exit_layer, lengths, kv_cache, norm_gain, w_qkv, w_out):
    devices = lax.axis_size("section")
    index = lax.axis_index("section")
    shards = max(2, devices // 4)
    cycle_size = devices // shards
    segment_bits = cycle_size.bit_length() - 1
    shard_bits = shards.bit_length() - 1
    segment_index = index // shards
    shard_index = index % shards
    own_blocks = hidden[0]
    gain_row = norm_gain[0].astype(jnp.float32)
    proj_weight = w_qkv[0]
    out_weight = w_out[0]
    cache_all = kv_cache[0]
    query_width = out_weight.shape[0]
    head_size = (proj_weight.shape[1] - query_width) // 2
    heads = query_width // head_size
    quarter = proj_weight.shape[0]
    total_width = quarter * shards
    group_rows = BLOCK // shards
    rounds = MICRO // cycle_size
    context = cache_all.shape[1]
    positions = jnp.arange(context, dtype=jnp.int32)
    blank_block = jnp.zeros((BLOCK, quarter), jnp.bfloat16)

    def advance(carry, microstep):
        incoming, arriving, records = carry
        micro_index = microstep - segment_index
        in_range = (micro_index >= 0) & (micro_index < MICRO)
        slot = jnp.clip(micro_index, 0, MICRO - 1)
        on_turn = microstep % cycle_size == 0
        local_slot = jnp.minimum(microstep // cycle_size, rounds - 1)
        own_block = lax.dynamic_slice_in_dim(own_blocks, local_slot * BLOCK, BLOCK, 0)
        exit_rows = lax.dynamic_slice_in_dim(exit_layer, slot * BLOCK, BLOCK)
        own_lengths = lax.dynamic_slice_in_dim(
            lengths, slot * BLOCK + shard_index * group_rows, group_rows
        )
        own_cache = lax.dynamic_slice_in_dim(cache_all, slot * group_rows, group_rows, 0)
        first_input = jnp.where(on_turn, own_block, arriving)
        entering = jnp.where(segment_index == 0, first_input, incoming)
        active = exit_rows > segment_index
        gate = in_range & (jnp.sum(active.astype(jnp.int32)) > 0)

        def local_partials():
            widened = entering.astype(jnp.float32)
            scaled = (widened * gain_row).astype(jnp.bfloat16)
            return (
                jnp.dot(scaled, proj_weight, preferred_element_type=jnp.float32),
                jnp.sum(widened * widened, axis=1),
            )

        def no_partials():
            return (
                jnp.zeros((BLOCK, proj_weight.shape[1]), jnp.float32),
                jnp.zeros((BLOCK,), jnp.float32),
            )

        partial_proj, partial_squares = lax.cond(gate, local_partials, no_partials)
        kept = (partial_proj, partial_squares)
        for level in range(shard_bits):
            bit = shard_bits - 1 - level
            upper = index >> bit & 1
            halves = tuple(
                (piece.reshape((2, piece.shape[0] // 2) + piece.shape[1:]) for piece in kept)
            )
            keep = tuple((jnp.where(upper == 1, half[1], half[0]) for half in halves))
            send = tuple((jnp.where(upper == 1, half[0], half[1]) for half in halves))
            received = partner(send, "section", bit)
            kept = tuple((first + second for first, second in zip(keep, received)))
        own_proj, own_squares = kept

        def local_attention():
            fitted = own_proj * lax.rsqrt(own_squares / total_width + EPSILON)[:, None]
            query = (fitted[:, :query_width] * (1.0 / math.sqrt(head_size))).astype(jnp.bfloat16)
            query = query.reshape(group_rows, heads, head_size)
            key_new = fitted[:, query_width : query_width + head_size].astype(jnp.bfloat16)
            value_new = fitted[:, query_width + head_size :].astype(jnp.bfloat16)
            scores = jnp.einsum(
                "rhd,rcd->rhc",
                query,
                own_cache[:, :, :head_size],
                preferred_element_type=jnp.float32,
            )
            own = jnp.einsum("rhd,rd->rh", query, key_new, preferred_element_type=jnp.float32)
            usable = (positions[None, :] < own_lengths[:, None])[:, None, :]
            scores = jnp.where(usable, scores, NEGATIVE)
            row_top = jnp.maximum(jnp.max(scores, axis=-1), own)
            raw = jnp.where(usable, jnp.exp(scores - row_top[:, :, None]), jnp.float32(0.0))
            raw_own = jnp.exp(own - row_top)
            total = jnp.sum(raw, axis=-1) + raw_own
            weights = (raw / total[:, :, None]).astype(jnp.bfloat16)
            own_weight = (raw_own / total).astype(jnp.bfloat16)
            attended = jnp.einsum(
                "rhc,rcd->rhd",
                weights,
                own_cache[:, :, head_size:],
                preferred_element_type=jnp.float32,
            )
            attended = (
                attended
                + own_weight.astype(jnp.float32)[:, :, None]
                * value_new.astype(jnp.float32)[:, None, :]
            )
            return attended.astype(jnp.bfloat16).reshape(group_rows, query_width)

        def no_attention():
            return jnp.zeros((group_rows, query_width), jnp.bfloat16)

        collected = lax.cond(gate, local_attention, no_attention)
        for level in range(shard_bits):
            bit = level
            other = partner(collected, "section", bit)
            upper = index >> bit & 1
            collected = jnp.where(
                upper == 1,
                jnp.concatenate([other, collected], 0),
                jnp.concatenate([collected, other], 0),
            )

        def local_update():
            branch_out = jnp.dot(collected, out_weight, preferred_element_type=jnp.float32)
            updated = (entering.astype(jnp.float32) + branch_out).astype(jnp.bfloat16)
            return jnp.where(active[:, None], updated, entering)

        def keep_state():
            return entering

        outgoing = lax.cond(gate, local_update, keep_state)
        leaving = in_range & (exit_rows == segment_index + 1)
        previous = lax.dynamic_slice_in_dim(records, slot * BLOCK, BLOCK, 0)
        records = lax.dynamic_update_slice_in_dim(
            records, jnp.where(leaving[:, None], outgoing, previous), slot * BLOCK, 0
        )
        relayed = jnp.where(on_turn & (segment_index > 0), own_block, arriving)
        incoming, arriving = shifted((outgoing, relayed), "section", shards)
        return ((incoming, arriving, records), None)

    start = (blank_block, blank_block, jnp.zeros((MICRO * BLOCK, quarter), jnp.bfloat16))
    carry, _ = lax.scan(advance, start, jnp.arange(MICRO + cycle_size - 1, dtype=jnp.int32))
    kept = carry[2]
    for level in range(segment_bits):
        bit = shard_bits + segment_bits - 1 - level
        upper = index >> bit & 1
        halves = kept.reshape(kept.shape[0], 2, kept.shape[1] // 2)
        keep = jnp.where(upper == 1, halves[:, 1], halves[:, 0])
        send = jnp.where(upper == 1, halves[:, 0], halves[:, 1])
        received = partner(send, "section", bit)
        kept = (keep.astype(jnp.float32) + received.astype(jnp.float32)).astype(jnp.bfloat16)
    return kept


def solution(mesh):
    return jax.shard_map(
        body,
        mesh=mesh,
        in_specs=(
            P("section", "blk", None),
            P("blk"),
            P("blk"),
            P("section", "blk", None, None),
            P("section", None),
            P("section", None, None),
            P("section", None, None),
        ),
        out_specs=P("blk", "section"),
        check_vma=False,
    )
```

profile of v0, /device:TPU:0, one launch (start us, length us, event | category | flops | bytes accessed | tf_op | source)
XLA Modules:
  0.0 422.3 jit_solution(11661736484920512998)
XLA Ops:
  3.3 369.8 %while.17 = (s32[]{:T(128)}, bf16[64,4096]{1,0:T(8,128)(2,1)S(1)}, bf16[64,4096]{1,0:T(8,128)(2,1)S(1)}, bf16[512,4096]{1,0:T(8,128)(2,1)}, s32[9]{0:T(128)S(1)}...) while((s32[]{:T(128)}, bf16[64,4096]{1,0:T(8,128)(2,1)S(1)}, ...), condition=%wide.region_11.12_spmd.clone, body=%wide.region_0.11_spmd.clone.sunk | while | flops 1214793728 | bytes 34297604 | solution.py:164
  9.8 6.2 %conditional.9 = (f32[32]{0:T(128)S(1)}, f32[32]{0:T(128)S(1)}, f32[32,1280]{1,0:T(8,128)S(1)}, f32[32,1280]{1,0:T(8,128)S(1)}) conditional(s32[]{:T(128)} %convert_element_type.122, () %tuple.95, (bf16[64,4096]{1,0:T(8,128)(2,1)S(1)}, f32[4096]{0:T(1024)S(1)}, bf16[4096,1280]{1,0:T(8,128)(2,1)}) %tuple.96), branch_computations={%region_2.2_spmd, %region_3.4_spmd} | conditional | flops 672661440 | bytes 12534560 | solution.py:83
  10.1 5.9 %fusion.4 = f32[64,1280]{1,0:T(8,128)S(1)} fusion(bf16[4096,1280]{1,0:T(8,128)(2,1)} %get-tuple-element.392, bf16[64,4096]{1,0:T(8,128)(2,1)S(1)} %get-tuple-element.390, f32[4096]{0:T(1024)S(1)} %get-tuple-element.391), kind=kOutput, calls=%fused_computation.5 | convolution fusion | flops 671875072 | bytes 11354112 | tf_op jit(solution)/shard_map/while/body/eval_jaxpr/cond/branch_1_fun/dot_general | solution.py:73
  16.1 3.0 collective-permute-start
  19.2 4.2 collective-permute-done.1
  23.5 3.8 conditional.10
  31.6 5.0 %conditional.11 = (bf16[64,4096]{1,0:T(8,128)(2,1)S(1)}) conditional(s32[]{:T(128)} %convert_element_type.122, bf16[64,4096]{1,0:T(8,128)(2,1)S(1)} %get-tuple-element.655, (pred[64]{0:T(512)(128)(4,1)S(1)}, bf16[64,4096]{1,0:T(8,128)(2,1)S(1)}, pred[]{:T(512)}, bf16[64,1024]{1,0:T(8,128)(2,1)S(1)}, bf16[64,1024]{1,0:T(8,128)(2,1)S(1)}, ...), branch_computations={%region_9.9_spmd, %region_10.10_spmd} | conditional | flops 537985024 | bytes 9699401 | solution.py:153
  31.6 5.0 %fusion.25 = bf16[64,4096]{1,0:T(8,128)(2,1)S(1)} fusion(bf16[64,4096]{1,0:T(8,128)(2,1)S(1)} %get-tuple-element.408, bf16[1024,4096]{1,0:T(8,128)(2,1)} %get-tuple-element.412, pred[64]{0:T(512)(128)(4,1)S(1)} %get-tuple-element.407, bf16[64,1024]{1,0:T(8,128)(2,1)S(1)} %get-tuple-element.410, bf16[64,1024]{1,0:T(8,128)(2,1)S(1)} %get-tuple-element.411, ...), kind=kOutput, calls=%fused_computation.39 | convolution fusion | flops 537985024 | bytes 9699393 | tf_op jit(solution)/shard_map/while/body/eval_jaxpr/cond/branch_1_fun/dot_general | solution.py:146
  38.8 10.1 %collective-permute-done.3 = bf16[64,4096]{1,0:T(8,128)(2,1)S(1)} collective-permute-done((bf16[64,4096]{1,0:T(8,128)(2,1)S(1)}, bf16[64,4096]{1,0:T(8,128)(2,1)S(1)}, u32[]{:S(2)}, u32[]{:S(2)}) %collective-permute-start.3) | collective-permute-done | bytes 524320 | tf_op jit(solution)/shard_map/while/body/eval_jaxpr/ppermute | solution.py:23
  55.4 6.2 %conditional.9 = (f32[32]{0:T(128)S(1)}, f32[32]{0:T(128)S(1)}, f32[32,1280]{1,0:T(8,128)S(1)}, f32[32,1280]{1,0:T(8,128)S(1)}) conditional(s32[]{:T(128)} %convert_element_type.122, () %tuple.95, (bf16[64,4096]{1,0:T(8,128)(2,1)S(1)}, f32[4096]{0:T(1024)S(1)}, bf16[4096,1280]{1,0:T(8,128)(2,1)}) %tuple.96), branch_computations={%region_2.2_spmd, %region_3.4_spmd} | conditional | flops 672661440 | bytes 12534560 | solution.py:83
  55.6 5.9 %fusion.4 = f32[64,1280]{1,0:T(8,128)S(1)} fusion(bf16[4096,1280]{1,0:T(8,128)(2,1)} %get-tuple-element.392, bf16[64,4096]{1,0:T(8,128)(2,1)S(1)} %get-tuple-element.390, f32[4096]{0:T(1024)S(1)} %get-tuple-element.391), kind=kOutput, calls=%fused_computation.5 | convolution fusion | flops 671875072 | bytes 11354112 | tf_op jit(solution)/shard_map/while/body/eval_jaxpr/cond/branch_1_fun/dot_general | solution.py:73
  64.0 3.1 collective-permute-done.1
  67.1 3.8 conditional.10
  75.3 5.0 %conditional.11 = (bf16[64,4096]{1,0:T(8,128)(2,1)S(1)}) conditional(s32[]{:T(128)} %convert_element_type.122, bf16[64,4096]{1,0:T(8,128)(2,1)S(1)} %get-tuple-element.655, (pred[64]{0:T(512)(128)(4,1)S(1)}, bf16[64,4096]{1,0:T(8,128)(2,1)S(1)}, pred[]{:T(512)}, bf16[64,1024]{1,0:T(8,128)(2,1)S(1)}, bf16[64,1024]{1,0:T(8,128)(2,1)S(1)}, ...), branch_computations={%region_9.9_spmd, %region_10.10_spmd} | conditional | flops 537985024 | bytes 9699401 | solution.py:153
  75.3 5.0 %fusion.25 = bf16[64,4096]{1,0:T(8,128)(2,1)S(1)} fusion(bf16[64,4096]{1,0:T(8,128)(2,1)S(1)} %get-tuple-element.408, bf16[1024,4096]{1,0:T(8,128)(2,1)} %get-tuple-element.412, pred[64]{0:T(512)(128)(4,1)S(1)} %get-tuple-element.407, bf16[64,1024]{1,0:T(8,128)(2,1)S(1)} %get-tuple-element.410, bf16[64,1024]{1,0:T(8,128)(2,1)S(1)} %get-tuple-element.411, ...), kind=kOutput, calls=%fused_computation.39 | convolution fusion | flops 537985024 | bytes 9699393 | tf_op jit(solution)/shard_map/while/body/eval_jaxpr/cond/branch_1_fun/dot_general | solution.py:146
  82.7 7.0 %collective-permute-done.3 = bf16[64,4096]{1,0:T(8,128)(2,1)S(1)} collective-permute-done((bf16[64,4096]{1,0:T(8,128)(2,1)S(1)}, bf16[64,4096]{1,0:T(8,128)(2,1)S(1)}, u32[]{:S(2)}, u32[]{:S(2)}) %collective-permute-start.3) | collective-permute-done | bytes 524320 | tf_op jit(solution)/shard_map/while/body/eval_jaxpr/ppermute | solution.py:23
  96.2 6.2 %conditional.9 = (f32[32]{0:T(128)S(1)}, f32[32]{0:T(128)S(1)}, f32[32,1280]{1,0:T(8,128)S(1)}, f32[32,1280]{1,0:T(8,128)S(1)}) conditional(s32[]{:T(128)} %convert_element_type.122, () %tuple.95, (bf16[64,4096]{1,0:T(8,128)(2,1)S(1)}, f32[4096]{0:T(1024)S(1)}, bf16[4096,1280]{1,0:T(8,128)(2,1)}) %tuple.96), branch_computations={%region_2.2_spmd, %region_3.4_spmd} | conditional | flops 672661440 | bytes 12534560 | solution.py:83
  96.4 5.9 %fusion.4 = f32[64,1280]{1,0:T(8,128)S(1)} fusion(bf16[4096,1280]{1,0:T(8,128)(2,1)} %get-tuple-element.392, bf16[64,4096]{1,0:T(8,128)(2,1)S(1)} %get-tuple-element.390, f32[4096]{0:T(1024)S(1)} %get-tuple-element.391), kind=kOutput, calls=%fused_computation.5 | convolution fusion | flops 671875072 | bytes 11354112 | tf_op jit(solution)/shard_map/while/body/eval_jaxpr/cond/branch_1_fun/dot_general | solution.py:73
  105.1 2.8 collective-permute-done.1
  108.0 3.8 conditional.10
  116.1 5.0 %conditional.11 = (bf16[64,4096]{1,0:T(8,128)(2,1)S(1)}) conditional(s32[]{:T(128)} %convert_element_type.122, bf16[64,4096]{1,0:T(8,128)(2,1)S(1)} %get-tuple-element.655, (pred[64]{0:T(512)(128)(4,1)S(1)}, bf16[64,4096]{1,0:T(8,128)(2,1)S(1)}, pred[]{:T(512)}, bf16[64,1024]{1,0:T(8,128)(2,1)S(1)}, bf16[64,1024]{1,0:T(8,128)(2,1)S(1)}, ...), branch_computations={%region_9.9_spmd, %region_10.10_spmd} | conditional | flops 537985024 | bytes 9699401 | solution.py:153
  116.1 5.0 %fusion.25 = bf16[64,4096]{1,0:T(8,128)(2,1)S(1)} fusion(bf16[64,4096]{1,0:T(8,128)(2,1)S(1)} %get-tuple-element.408, bf16[1024,4096]{1,0:T(8,128)(2,1)} %get-tuple-element.412, pred[64]{0:T(512)(128)(4,1)S(1)} %get-tuple-element.407, bf16[64,1024]{1,0:T(8,128)(2,1)S(1)} %get-tuple-element.410, bf16[64,1024]{1,0:T(8,128)(2,1)S(1)} %get-tuple-element.411, ...), kind=kOutput, calls=%fused_computation.39 | convolution fusion | flops 537985024 | bytes 9699393 | tf_op jit(solution)/shard_map/while/body/eval_jaxpr/cond/branch_1_fun/dot_general | solution.py:146
  123.8 6.6 %collective-permute-done.3 = bf16[64,4096]{1,0:T(8,128)(2,1)S(1)} collective-permute-done((bf16[64,4096]{1,0:T(8,128)(2,1)S(1)}, bf16[64,4096]{1,0:T(8,128)(2,1)S(1)}, u32[]{:S(2)}, u32[]{:S(2)}) %collective-permute-start.3) | collective-permute-done | bytes 524320 | tf_op jit(solution)/shard_map/while/body/eval_jaxpr/ppermute | solution.py:23
  136.9 6.2 %conditional.9 = (f32[32]{0:T(128)S(1)}, f32[32]{0:T(128)S(1)}, f32[32,1280]{1,0:T(8,128)S(1)}, f32[32,1280]{1,0:T(8,128)S(1)}) conditional(s32[]{:T(128)} %convert_element_type.122, () %tuple.95, (bf16[64,4096]{1,0:T(8,128)(2,1)S(1)}, f32[4096]{0:T(1024)S(1)}, bf16[4096,1280]{1,0:T(8,128)(2,1)}) %tuple.96), branch_computations={%region_2.2_spmd, %region_3.4_spmd} | conditional | flops 672661440 | bytes 12534560 | solution.py:83
  137.1 5.9 %fusion.4 = f32[64,1280]{1,0:T(8,128)S(1)} fusion(bf16[4096,1280]{1,0:T(8,128)(2,1)} %get-tuple-element.392, bf16[64,4096]{1,0:T(8,128)(2,1)S(1)} %get-tuple-element.390, f32[4096]{0:T(1024)S(1)} %get-tuple-element.391), kind=kOutput, calls=%fused_computation.5 | convolution fusion | flops 671875072 | bytes 11354112 | tf_op jit(solution)/shard_map/while/body/eval_jaxpr/cond/branch_1_fun/dot_general | solution.py:73
  145.8 2.9 collective-permute-done.1
  148.7 3.8 conditional.10
  156.9 5.0 %conditional.11 = (bf16[64,4096]{1,0:T(8,128)(2,1)S(1)}) conditional(s32[]{:T(128)} %convert_element_type.122, bf16[64,4096]{1,0:T(8,128)(2,1)S(1)} %get-tuple-element.655, (pred[64]{0:T(512)(128)(4,1)S(1)}, bf16[64,4096]{1,0:T(8,128)(2,1)S(1)}, pred[]{:T(512)}, bf16[64,1024]{1,0:T(8,128)(2,1)S(1)}, bf16[64,1024]{1,0:T(8,128)(2,1)S(1)}, ...), branch_computations={%region_9.9_spmd, %region_10.10_spmd} | conditional | flops 537985024 | bytes 9699401 | solution.py:153
  156.9 5.0 %fusion.25 = bf16[64,4096]{1,0:T(8,128)(2,1)S(1)} fusion(bf16[64,4096]{1,0:T(8,128)(2,1)S(1)} %get-tuple-element.408, bf16[1024,4096]{1,0:T(8,128)(2,1)} %get-tuple-element.412, pred[64]{0:T(512)(128)(4,1)S(1)} %get-tuple-element.407, bf16[64,1024]{1,0:T(8,128)(2,1)S(1)} %get-tuple-element.410, bf16[64,1024]{1,0:T(8,128)(2,1)S(1)} %get-tuple-element.411, ...), kind=kOutput, calls=%fused_computation.39 | convolution fusion | flops 537985024 | bytes 9699393 | tf_op jit(solution)/shard_map/while/body/eval_jaxpr/cond/branch_1_fun/dot_general | solution.py:146
  164.5 6.6 %collective-permute-done.3 = bf16[64,4096]{1,0:T(8,128)(2,1)S(1)} collective-permute-done((bf16[64,4096]{1,0:T(8,128)(2,1)S(1)}, bf16[64,4096]{1,0:T(8,128)(2,1)S(1)}, u32[]{:S(2)}, u32[]{:S(2)}) %collective-permute-start.3) | collective-permute-done | bytes 524320 | tf_op jit(solution)/shard_map/while/body/eval_jaxpr/ppermute | solution.py:23
  177.7 6.2 %conditional.9 = (f32[32]{0:T(128)S(1)}, f32[32]{0:T(128)S(1)}, f32[32,1280]{1,0:T(8,128)S(1)}, f32[32,1280]{1,0:T(8,128)S(1)}) conditional(s32[]{:T(128)} %convert_element_type.122, () %tuple.95, (bf16[64,4096]{1,0:T(8,128)(2,1)S(1)}, f32[4096]{0:T(1024)S(1)}, bf16[4096,1280]{1,0:T(8,128)(2,1)}) %tuple.96), branch_computations={%region_2.2_spmd, %region_3.4_spmd} | conditional | flops 672661440 | bytes 12534560 | solution.py:83
  177.9 5.9 %fusion.4 = f32[64,1280]{1,0:T(8,128)S(1)} fusion(bf16[4096,1280]{1,0:T(8,128)(2,1)} %get-tuple-element.392, bf16[64,4096]{1,0:T(8,128)(2,1)S(1)} %get-tuple-element.390, f32[4096]{0:T(1024)S(1)} %get-tuple-element.391), kind=kOutput, calls=%fused_computation.5 | convolution fusion | flops 671875072 | bytes 11354112 | tf_op jit(solution)/shard_map/while/body/eval_jaxpr/cond/branch_1_fun/dot_general | solution.py:73
  186.5 2.9 collective-permute-done.1
  189.5 3.8 conditional.10
  197.6 5.0 %conditional.11 = (bf16[64,4096]{1,0:T(8,128)(2,1)S(1)}) conditional(s32[]{:T(128)} %convert_element_type.122, bf16[64,4096]{1,0:T(8,128)(2,1)S(1)} %get-tuple-element.655, (pred[64]{0:T(512)(128)(4,1)S(1)}, bf16[64,4096]{1,0:T(8,128)(2,1)S(1)}, pred[]{:T(512)}, bf16[64,1024]{1,0:T(8,128)(2,1)S(1)}, bf16[64,1024]{1,0:T(8,128)(2,1)S(1)}, ...), branch_computations={%region_9.9_spmd, %region_10.10_spmd} | conditional | flops 537985024 | bytes 9699401 | solution.py:153
  197.6 5.0 %fusion.25 = bf16[64,4096]{1,0:T(8,128)(2,1)S(1)} fusion(bf16[64,4096]{1,0:T(8,128)(2,1)S(1)} %get-tuple-element.408, bf16[1024,4096]{1,0:T(8,128)(2,1)} %get-tuple-element.412, pred[64]{0:T(512)(128)(4,1)S(1)} %get-tuple-element.407, bf16[64,1024]{1,0:T(8,128)(2,1)S(1)} %get-tuple-element.410, bf16[64,1024]{1,0:T(8,128)(2,1)S(1)} %get-tuple-element.411, ...), kind=kOutput, calls=%fused_computation.39 | convolution fusion | flops 537985024 | bytes 9699393 | tf_op jit(solution)/shard_map/while/body/eval_jaxpr/cond/branch_1_fun/dot_general | solution.py:146
  205.2 6.6 %collective-permute-done.3 = bf16[64,4096]{1,0:T(8,128)(2,1)S(1)} collective-permute-done((bf16[64,4096]{1,0:T(8,128)(2,1)S(1)}, bf16[64,4096]{1,0:T(8,128)(2,1)S(1)}, u32[]{:S(2)}, u32[]{:S(2)}) %collective-permute-start.3) | collective-permute-done | bytes 524320 | tf_op jit(solution)/shard_map/while/body/eval_jaxpr/ppermute | solution.py:23
  218.4 6.2 %conditional.9 = (f32[32]{0:T(128)S(1)}, f32[32]{0:T(128)S(1)}, f32[32,1280]{1,0:T(8,128)S(1)}, f32[32,1280]{1,0:T(8,128)S(1)}) conditional(s32[]{:T(128)} %convert_element_type.122, () %tuple.95, (bf16[64,4096]{1,0:T(8,128)(2,1)S(1)}, f32[4096]{0:T(1024)S(1)}, bf16[4096,1280]{1,0:T(8,128)(2,1)}) %tuple.96), branch_computations={%region_2.2_spmd, %region_3.4_spmd} | conditional | flops 672661440 | bytes 12534560 | solution.py:83
  218.6 5.9 %fusion.4 = f32[64,1280]{1,0:T(8,128)S(1)} fusion(bf16[4096,1280]{1,0:T(8,128)(2,1)} %get-tuple-element.392, bf16[64,4096]{1,0:T(8,128)(2,1)S(1)} %get-tuple-element.390, f32[4096]{0:T(1024)S(1)} %get-tuple-element.391), kind=kOutput, calls=%fused_computation.5 | convolution fusion | flops 671875072 | bytes 11354112 | tf_op jit(solution)/shard_map/while/body/eval_jaxpr/cond/branch_1_fun/dot_general | solution.py:73
  227.2 2.9 collective-permute-done.1
  230.2 3.8 conditional.10
  238.3 5.0 %conditional.11 = (bf16[64,4096]{1,0:T(8,128)(2,1)S(1)}) conditional(s32[]{:T(128)} %convert_element_type.122, bf16[64,4096]{1,0:T(8,128)(2,1)S(1)} %get-tuple-element.655, (pred[64]{0:T(512)(128)(4,1)S(1)}, bf16[64,4096]{1,0:T(8,128)(2,1)S(1)}, pred[]{:T(512)}, bf16[64,1024]{1,0:T(8,128)(2,1)S(1)}, bf16[64,1024]{1,0:T(8,128)(2,1)S(1)}, ...), branch_computations={%region_9.9_spmd, %region_10.10_spmd} | conditional | flops 537985024 | bytes 9699401 | solution.py:153
  238.3 5.0 %fusion.25 = bf16[64,4096]{1,0:T(8,128)(2,1)S(1)} fusion(bf16[64,4096]{1,0:T(8,128)(2,1)S(1)} %get-tuple-element.408, bf16[1024,4096]{1,0:T(8,128)(2,1)} %get-tuple-element.412, pred[64]{0:T(512)(128)(4,1)S(1)} %get-tuple-element.407, bf16[64,1024]{1,0:T(8,128)(2,1)S(1)} %get-tuple-element.410, bf16[64,1024]{1,0:T(8,128)(2,1)S(1)} %get-tuple-element.411, ...), kind=kOutput, calls=%fused_computation.39 | convolution fusion | flops 537985024 | bytes 9699393 | tf_op jit(solution)/shard_map/while/body/eval_jaxpr/cond/branch_1_fun/dot_general | solution.py:146
  245.9 6.6 %collective-permute-done.3 = bf16[64,4096]{1,0:T(8,128)(2,1)S(1)} collective-permute-done((bf16[64,4096]{1,0:T(8,128)(2,1)S(1)}, bf16[64,4096]{1,0:T(8,128)(2,1)S(1)}, u32[]{:S(2)}, u32[]{:S(2)}) %collective-permute-start.3) | collective-permute-done | bytes 524320 | tf_op jit(solution)/shard_map/while/body/eval_jaxpr/ppermute | solution.py:23
  259.1 6.2 %conditional.9 = (f32[32]{0:T(128)S(1)}, f32[32]{0:T(128)S(1)}, f32[32,1280]{1,0:T(8,128)S(1)}, f32[32,1280]{1,0:T(8,128)S(1)}) conditional(s32[]{:T(128)} %convert_element_type.122, () %tuple.95, (bf16[64,4096]{1,0:T(8,128)(2,1)S(1)}, f32[4096]{0:T(1024)S(1)}, bf16[4096,1280]{1,0:T(8,128)(2,1)}) %tuple.96), branch_computations={%region_2.2_spmd, %region_3.4_spmd} | conditional | flops 672661440 | bytes 12534560 | solution.py:83
  259.3 5.9 %fusion.4 = f32[64,1280]{1,0:T(8,128)S(1)} fusion(bf16[4096,1280]{1,0:T(8,128)(2,1)} %get-tuple-element.392, bf16[64,4096]{1,0:T(8,128)(2,1)S(1)} %get-tuple-element.390, f32[4096]{0:T(1024)S(1)} %get-tuple-element.391), kind=kOutput, calls=%fused_computation.5 | convolution fusion | flops 671875072 | bytes 11354112 | tf_op jit(solution)/shard_map/while/body/eval_jaxpr/cond/branch_1_fun/dot_general | solution.py:73
  267.9 2.9 collective-permute-done.1
  270.9 3.8 conditional.10
  279.0 5.0 %conditional.11 = (bf16[64,4096]{1,0:T(8,128)(2,1)S(1)}) conditional(s32[]{:T(128)} %convert_element_type.122, bf16[64,4096]{1,0:T(8,128)(2,1)S(1)} %get-tuple-element.655, (pred[64]{0:T(512)(128)(4,1)S(1)}, bf16[64,4096]{1,0:T(8,128)(2,1)S(1)}, pred[]{:T(512)}, bf16[64,1024]{1,0:T(8,128)(2,1)S(1)}, bf16[64,1024]{1,0:T(8,128)(2,1)S(1)}, ...), branch_computations={%region_9.9_spmd, %region_10.10_spmd} | conditional | flops 537985024 | bytes 9699401 | solution.py:153
  279.0 5.0 %fusion.25 = bf16[64,4096]{1,0:T(8,128)(2,1)S(1)} fusion(bf16[64,4096]{1,0:T(8,128)(2,1)S(1)} %get-tuple-element.408, bf16[1024,4096]{1,0:T(8,128)(2,1)} %get-tuple-element.412, pred[64]{0:T(512)(128)(4,1)S(1)} %get-tuple-element.407, bf16[64,1024]{1,0:T(8,128)(2,1)S(1)} %get-tuple-element.410, bf16[64,1024]{1,0:T(8,128)(2,1)S(1)} %get-tuple-element.411, ...), kind=kOutput, calls=%fused_computation.39 | convolution fusion | flops 537985024 | bytes 9699393 | tf_op jit(solution)/shard_map/while/body/eval_jaxpr/cond/branch_1_fun/dot_general | solution.py:146
  286.6 6.6 %collective-permute-done.3 = bf16[64,4096]{1,0:T(8,128)(2,1)S(1)} collective-permute-done((bf16[64,4096]{1,0:T(8,128)(2,1)S(1)}, bf16[64,4096]{1,0:T(8,128)(2,1)S(1)}, u32[]{:S(2)}, u32[]{:S(2)}) %collective-permute-start.3) | collective-permute-done | bytes 524320 | tf_op jit(solution)/shard_map/while/body/eval_jaxpr/ppermute | solution.py:23
  299.8 6.2 %conditional.9 = (f32[32]{0:T(128)S(1)}, f32[32]{0:T(128)S(1)}, f32[32,1280]{1,0:T(8,128)S(1)}, f32[32,1280]{1,0:T(8,128)S(1)}) conditional(s32[]{:T(128)} %convert_element_type.122, () %tuple.95, (bf16[64,4096]{1,0:T(8,128)(2,1)S(1)}, f32[4096]{0:T(1024)S(1)}, bf16[4096,1280]{1,0:T(8,128)(2,1)}) %tuple.96), branch_computations={%region_2.2_spmd, %region_3.4_spmd} | conditional | flops 672661440 | bytes 12534560 | solution.py:83
  300.0 5.9 %fusion.4 = f32[64,1280]{1,0:T(8,128)S(1)} fusion(bf16[4096,1280]{1,0:T(8,128)(2,1)} %get-tuple-element.392, bf16[64,4096]{1,0:T(8,128)(2,1)S(1)} %get-tuple-element.390, f32[4096]{0:T(1024)S(1)} %get-tuple-element.391), kind=kOutput, calls=%fused_computation.5 | convolution fusion | flops 671875072 | bytes 11354112 | tf_op jit(solution)/shard_map/while/body/eval_jaxpr/cond/branch_1_fun/dot_general | solution.py:73
  308.7 2.9 collective-permute-done.1
  311.6 3.8 conditional.10
  319.7 5.0 %conditional.11 = (bf16[64,4096]{1,0:T(8,128)(2,1)S(1)}) conditional(s32[]{:T(128)} %convert_element_type.122, bf16[64,4096]{1,0:T(8,128)(2,1)S(1)} %get-tuple-element.655, (pred[64]{0:T(512)(128)(4,1)S(1)}, bf16[64,4096]{1,0:T(8,128)(2,1)S(1)}, pred[]{:T(512)}, bf16[64,1024]{1,0:T(8,128)(2,1)S(1)}, bf16[64,1024]{1,0:T(8,128)(2,1)S(1)}, ...), branch_computations={%region_9.9_spmd, %region_10.10_spmd} | conditional | flops 537985024 | bytes 9699401 | solution.py:153
  319.7 5.0 %fusion.25 = bf16[64,4096]{1,0:T(8,128)(2,1)S(1)} fusion(bf16[64,4096]{1,0:T(8,128)(2,1)S(1)} %get-tuple-element.408, bf16[1024,4096]{1,0:T(8,128)(2,1)} %get-tuple-element.412, pred[64]{0:T(512)(128)(4,1)S(1)} %get-tuple-element.407, bf16[64,1024]{1,0:T(8,128)(2,1)S(1)} %get-tuple-element.410, bf16[64,1024]{1,0:T(8,128)(2,1)S(1)} %get-tuple-element.411, ...), kind=kOutput, calls=%fused_computation.39 | convolution fusion | flops 537985024 | bytes 9699393 | tf_op jit(solution)/shard_map/while/body/eval_jaxpr/cond/branch_1_fun/dot_general | solution.py:146
  327.3 6.7 %collective-permute-done.3 = bf16[64,4096]{1,0:T(8,128)(2,1)S(1)} collective-permute-done((bf16[64,4096]{1,0:T(8,128)(2,1)S(1)}, bf16[64,4096]{1,0:T(8,128)(2,1)S(1)}, u32[]{:S(2)}, u32[]{:S(2)}) %collective-permute-start.3) | collective-permute-done | bytes 524320 | tf_op jit(solution)/shard_map/while/body/eval_jaxpr/ppermute | solution.py:23
  342.7 6.6 %collective-permute-start.4 = (bf16[64,4096]{1,0:T(8,128)(2,1)S(1)}, bf16[64,4096]{1,0:T(8,128)(2,1)S(1)}, u32[]{:S(2)}, u32[]{:S(2)}) collective-permute-start(bf16[64,4096]{1,0:T(8,128)(2,1)S(1)} %get-tuple-element.663), channel_id=1, source_target_pairs={{0,2},{1,3},{2,0},{3,1},{4,6},{5,7},{6,4},{7,5},{8,10},{9,11},{10,... | collective-permute-start | bytes 1572872 | tf_op jit(solution)/shard_map/while/body/eval_jaxpr/ppermute | solution.py:23
  350.9 2.8 collective-permute-done.2
  353.8 12.2 %collective-permute-start.3 = (bf16[64,4096]{1,0:T(8,128)(2,1)S(1)}, bf16[64,4096]{1,0:T(8,128)(2,1)S(1)}, u32[]{:S(2)}, u32[]{:S(2)}) collective-permute-start(bf16[64,4096]{1,0:T(8,128)(2,1)S(1)} %get-tuple-element.757), channel_id=1, source_target_pairs={{0,2},{1,3},{2,0},{3,1},{4,6},{5,7},{6,4},{7,5},{8,10},{9,11},{10,... | collective-permute-start | bytes 1572872 | tf_op jit(solution)/shard_map/while/body/eval_jaxpr/ppermute | solution.py:23
  368.0 5.1 %collective-permute-done.3 = bf16[64,4096]{1,0:T(8,128)(2,1)S(1)} collective-permute-done((bf16[64,4096]{1,0:T(8,128)(2,1)S(1)}, bf16[64,4096]{1,0:T(8,128)(2,1)S(1)}, u32[]{:S(2)}, u32[]{:S(2)}) %collective-permute-start.3) | collective-permute-done | bytes 524320 | tf_op jit(solution)/shard_map/while/body/eval_jaxpr/ppermute | solution.py:23
  373.2 6.5 %copy.8 = bf16[512,4096]{0,1:T(8,128)(2,1)} copy(bf16[512,4096]{1,0:T(8,128)(2,1)} %get-tuple-element.438) | data formatting | bytes 8388608 | tf_op jit(solution)/shard_map/while | solution.py:164
  384.3 34.6 %collective-permute-done.5 = bf16[512,2048]{0,1:T(8,128)(2,1)S(1)} collective-permute-done((bf16[512,2048]{0,1:T(8,128)(2,1)S(1)}, bf16[512,2048]{0,1:T(8,128)(2,1)S(1)}, u32[]{:S(2)}, u32[]{:S(2)}) %collective-permute-start.5) | collective-permute-done | bytes 2097184 | tf_op jit(solution)/shard_map/ppermute | solution.py:17
  (325 shorter events, 146.5 us)
Async XLA Ops:
  0.0 3.3 copy-start.1
  16.1 7.3 %collective-permute-start = (f32[32,1280]{1,0:T(8,128)S(1)}, f32[32,1280]{1,0:T(8,128)S(1)}, u32[]{:S(2)}, u32[]{:S(2)}) collective-permute-start(f32[32,1280]{1,0:T(8,128)S(1)} %broadcast_select_fusion.7), channel_id=1, source_target_pairs={{0,1},{1,0},{2,3},{3,2},{4,5},{5,4},{6,7},{7,6},{8,9},{9,8},{10,11... | collective-permute-start | bytes 491528 | tf_op jit(solution)/shard_map/while/body/eval_jaxpr/ppermute | solution.py:17
  19.1 4.3 %collective-permute-start.1 = (f32[32]{0:T(128)S(1)}, f32[32]{0:T(128)S(1)}, u32[]{:S(2)}, u32[]{:S(2)}) collective-permute-start(f32[32]{0:T(128)S(1)} %broadcast_select_fusion.8), channel_id=1, source_target_pairs={{0,1},{1,0},{2,3},{3,2},{4,5},{5,4},{6,7},{7,6},{8,9},{9,8},{10,11... | collective-permute-start | bytes 392 | tf_op jit(solution)/shard_map/while/body/eval_jaxpr/ppermute | solution.py:17
  19.2 19.5 %collective-permute-start.4 = (bf16[64,4096]{1,0:T(8,128)(2,1)S(1)}, bf16[64,4096]{1,0:T(8,128)(2,1)S(1)}, u32[]{:S(2)}, u32[]{:S(2)}) collective-permute-start(bf16[64,4096]{1,0:T(8,128)(2,1)S(1)} %get-tuple-element.663), channel_id=1, source_target_pairs={{0,2},{1,3},{2,0},{3,1},{4,6},{5,7},{6,4},{7,5},{8,10},{9,11},{10,... | collective-permute-start | bytes 1572872 | tf_op jit(solution)/shard_map/while/body/eval_jaxpr/ppermute | solution.py:23
  27.3 4.3 %collective-permute-start.2 = (bf16[32,1024]{1,0:T(8,128)(2,1)S(1)}, bf16[32,1024]{1,0:T(8,128)(2,1)S(1)}, u32[]{:S(2)}, u32[]{:S(2)}) collective-permute-start(bf16[32,1024]{1,0:T(8,128)(2,1)S(1)} %get-tuple-element.756), channel_id=1, source_target_pairs={{0,1},{1,0},{2,3},{3,2},{4,5},{5,4},{6,7},{7,6},{8,9},{9,8},{10,11... | collective-permute-start | bytes 196616 | tf_op jit(solution)/shard_map/while/body/eval_jaxpr/ppermute | solution.py:17
  36.6 12.2 %collective-permute-start.3 = (bf16[64,4096]{1,0:T(8,128)(2,1)S(1)}, bf16[64,4096]{1,0:T(8,128)(2,1)S(1)}, u32[]{:S(2)}, u32[]{:S(2)}) collective-permute-start(bf16[64,4096]{1,0:T(8,128)(2,1)S(1)} %get-tuple-element.757), channel_id=1, source_target_pairs={{0,2},{1,3},{2,0},{3,1},{4,6},{5,7},{6,4},{7,5},{8,10},{9,11},{10,... | collective-permute-start | bytes 1572872 | tf_op jit(solution)/shard_map/while/body/eval_jaxpr/ppermute | solution.py:23
  61.6 5.5 %collective-permute-start = (f32[32,1280]{1,0:T(8,128)S(1)}, f32[32,1280]{1,0:T(8,128)S(1)}, u32[]{:S(2)}, u32[]{:S(2)}) collective-permute-start(f32[32,1280]{1,0:T(8,128)S(1)} %broadcast_select_fusion.7), channel_id=1, source_target_pairs={{0,1},{1,0},{2,3},{3,2},{4,5},{5,4},{6,7},{7,6},{8,9},{9,8},{10,11... | collective-permute-start | bytes 491528 | tf_op jit(solution)/shard_map/while/body/eval_jaxpr/ppermute | solution.py:17
  63.2 3.9 collective-permute-start.1
  63.7 19.0 %collective-permute-start.4 = (bf16[64,4096]{1,0:T(8,128)(2,1)S(1)}, bf16[64,4096]{1,0:T(8,128)(2,1)S(1)}, u32[]{:S(2)}, u32[]{:S(2)}) collective-permute-start(bf16[64,4096]{1,0:T(8,128)(2,1)S(1)} %get-tuple-element.663), channel_id=1, source_target_pairs={{0,2},{1,3},{2,0},{3,1},{4,6},{5,7},{6,4},{7,5},{8,10},{9,11},{10,... | collective-permute-start | bytes 1572872 | tf_op jit(solution)/shard_map/while/body/eval_jaxpr/ppermute | solution.py:23
  70.9 4.3 %collective-permute-start.2 = (bf16[32,1024]{1,0:T(8,128)(2,1)S(1)}, bf16[32,1024]{1,0:T(8,128)(2,1)S(1)}, u32[]{:S(2)}, u32[]{:S(2)}) collective-permute-start(bf16[32,1024]{1,0:T(8,128)(2,1)S(1)} %get-tuple-element.756), channel_id=1, source_target_pairs={{0,1},{1,0},{2,3},{3,2},{4,5},{5,4},{6,7},{7,6},{8,9},{9,8},{10,11... | collective-permute-start | bytes 196616 | tf_op jit(solution)/shard_map/while/body/eval_jaxpr/ppermute | solution.py:17
  80.3 9.4 %collective-permute-start.3 = (bf16[64,4096]{1,0:T(8,128)(2,1)S(1)}, bf16[64,4096]{1,0:T(8,128)(2,1)S(1)}, u32[]{:S(2)}, u32[]{:S(2)}) collective-permute-start(bf16[64,4096]{1,0:T(8,128)(2,1)S(1)} %get-tuple-element.757), channel_id=1, source_target_pairs={{0,2},{1,3},{2,0},{3,1},{4,6},{5,7},{6,4},{7,5},{8,10},{9,11},{10,... | collective-permute-start | bytes 1572872 | tf_op jit(solution)/shard_map/while/body/eval_jaxpr/ppermute | solution.py:23
  102.5 5.5 %collective-permute-start = (f32[32,1280]{1,0:T(8,128)S(1)}, f32[32,1280]{1,0:T(8,128)S(1)}, u32[]{:S(2)}, u32[]{:S(2)}) collective-permute-start(f32[32,1280]{1,0:T(8,128)S(1)} %broadcast_select_fusion.7), channel_id=1, source_target_pairs={{0,1},{1,0},{2,3},{3,2},{4,5},{5,4},{6,7},{7,6},{8,9},{9,8},{10,11... | collective-permute-start | bytes 491528 | tf_op jit(solution)/shard_map/while/body/eval_jaxpr/ppermute | solution.py:17
  103.9 4.0 collective-permute-start.1
  104.5 19.3 %collective-permute-start.4 = (bf16[64,4096]{1,0:T(8,128)(2,1)S(1)}, bf16[64,4096]{1,0:T(8,128)(2,1)S(1)}, u32[]{:S(2)}, u32[]{:S(2)}) collective-permute-start(bf16[64,4096]{1,0:T(8,128)(2,1)S(1)} %get-tuple-element.663), channel_id=1, source_target_pairs={{0,2},{1,3},{2,0},{3,1},{4,6},{5,7},{6,4},{7,5},{8,10},{9,11},{10,... | collective-permute-start | bytes 1572872 | tf_op jit(solution)/shard_map/while/body/eval_jaxpr/ppermute | solution.py:23
  111.7 4.3 %collective-permute-start.2 = (bf16[32,1024]{1,0:T(8,128)(2,1)S(1)}, bf16[32,1024]{1,0:T(8,128)(2,1)S(1)}, u32[]{:S(2)}, u32[]{:S(2)}) collective-permute-start(bf16[32,1024]{1,0:T(8,128)(2,1)S(1)} %get-tuple-element.756), channel_id=1, source_target_pairs={{0,1},{1,0},{2,3},{3,2},{4,5},{5,4},{6,7},{7,6},{8,9},{9,8},{10,11... | collective-permute-start | bytes 196616 | tf_op jit(solution)/shard_map/while/body/eval_jaxpr/ppermute | solution.py:17
  121.1 9.2 %collective-permute-start.3 = (bf16[64,4096]{1,0:T(8,128)(2,1)S(1)}, bf16[64,4096]{1,0:T(8,128)(2,1)S(1)}, u32[]{:S(2)}, u32[]{:S(2)}) collective-permute-start(bf16[64,4096]{1,0:T(8,128)(2,1)S(1)} %get-tuple-element.757), channel_id=1, source_target_pairs={{0,2},{1,3},{2,0},{3,1},{4,6},{5,7},{6,4},{7,5},{8,10},{9,11},{10,... | collective-permute-start | bytes 1572872 | tf_op jit(solution)/shard_map/while/body/eval_jaxpr/ppermute | solution.py:23
  143.2 5.6 %collective-permute-start = (f32[32,1280]{1,0:T(8,128)S(1)}, f32[32,1280]{1,0:T(8,128)S(1)}, u32[]{:S(2)}, u32[]{:S(2)}) collective-permute-start(f32[32,1280]{1,0:T(8,128)S(1)} %broadcast_select_fusion.7), channel_id=1, source_target_pairs={{0,1},{1,0},{2,3},{3,2},{4,5},{5,4},{6,7},{7,6},{8,9},{9,8},{10,11... | collective-permute-start | bytes 491528 | tf_op jit(solution)/shard_map/while/body/eval_jaxpr/ppermute | solution.py:17
  145.1 3.6 collective-permute-start.1
  145.3 19.3 %collective-permute-start.4 = (bf16[64,4096]{1,0:T(8,128)(2,1)S(1)}, bf16[64,4096]{1,0:T(8,128)(2,1)S(1)}, u32[]{:S(2)}, u32[]{:S(2)}) collective-permute-start(bf16[64,4096]{1,0:T(8,128)(2,1)S(1)} %get-tuple-element.663), channel_id=1, source_target_pairs={{0,2},{1,3},{2,0},{3,1},{4,6},{5,7},{6,4},{7,5},{8,10},{9,11},{10,... | collective-permute-start | bytes 1572872 | tf_op jit(solution)/shard_map/while/body/eval_jaxpr/ppermute | solution.py:23
  152.5 4.3 %collective-permute-start.2 = (bf16[32,1024]{1,0:T(8,128)(2,1)S(1)}, bf16[32,1024]{1,0:T(8,128)(2,1)S(1)}, u32[]{:S(2)}, u32[]{:S(2)}) collective-permute-start(bf16[32,1024]{1,0:T(8,128)(2,1)S(1)} %get-tuple-element.756), channel_id=1, source_target_pairs={{0,1},{1,0},{2,3},{3,2},{4,5},{5,4},{6,7},{7,6},{8,9},{9,8},{10,11... | collective-permute-start | bytes 196616 | tf_op jit(solution)/shard_map/while/body/eval_jaxpr/ppermute | solution.py:17
  161.9 9.2 %collective-permute-start.3 = (bf16[64,4096]{1,0:T(8,128)(2,1)S(1)}, bf16[64,4096]{1,0:T(8,128)(2,1)S(1)}, u32[]{:S(2)}, u32[]{:S(2)}) collective-permute-start(bf16[64,4096]{1,0:T(8,128)(2,1)S(1)} %get-tuple-element.757), channel_id=1, source_target_pairs={{0,2},{1,3},{2,0},{3,1},{4,6},{5,7},{6,4},{7,5},{8,10},{9,11},{10,... | collective-permute-start | bytes 1572872 | tf_op jit(solution)/shard_map/while/body/eval_jaxpr/ppermute | solution.py:23
  183.9 5.5 %collective-permute-start = (f32[32,1280]{1,0:T(8,128)S(1)}, f32[32,1280]{1,0:T(8,128)S(1)}, u32[]{:S(2)}, u32[]{:S(2)}) collective-permute-start(f32[32,1280]{1,0:T(8,128)S(1)} %broadcast_select_fusion.7), channel_id=1, source_target_pairs={{0,1},{1,0},{2,3},{3,2},{4,5},{5,4},{6,7},{7,6},{8,9},{9,8},{10,11... | collective-permute-start | bytes 491528 | tf_op jit(solution)/shard_map/while/body/eval_jaxpr/ppermute | solution.py:17
  185.8 3.6 collective-permute-start.1
  186.0 19.2 %collective-permute-start.4 = (bf16[64,4096]{1,0:T(8,128)(2,1)S(1)}, bf16[64,4096]{1,0:T(8,128)(2,1)S(1)}, u32[]{:S(2)}, u32[]{:S(2)}) collective-permute-start(bf16[64,4096]{1,0:T(8,128)(2,1)S(1)} %get-tuple-element.663), channel_id=1, source_target_pairs={{0,2},{1,3},{2,0},{3,1},{4,6},{5,7},{6,4},{7,5},{8,10},{9,11},{10,... | collective-permute-start | bytes 1572872 | tf_op jit(solution)/shard_map/while/body/eval_jaxpr/ppermute | solution.py:23
  193.2 4.3 %collective-permute-start.2 = (bf16[32,1024]{1,0:T(8,128)(2,1)S(1)}, bf16[32,1024]{1,0:T(8,128)(2,1)S(1)}, u32[]{:S(2)}, u32[]{:S(2)}) collective-permute-start(bf16[32,1024]{1,0:T(8,128)(2,1)S(1)} %get-tuple-element.756), channel_id=1, source_target_pairs={{0,1},{1,0},{2,3},{3,2},{4,5},{5,4},{6,7},{7,6},{8,9},{9,8},{10,11... | collective-permute-start | bytes 196616 | tf_op jit(solution)/shard_map/while/body/eval_jaxpr/ppermute | solution.py:17
  202.6 9.2 %collective-permute-start.3 = (bf16[64,4096]{1,0:T(8,128)(2,1)S(1)}, bf16[64,4096]{1,0:T(8,128)(2,1)S(1)}, u32[]{:S(2)}, u32[]{:S(2)}) collective-permute-start(bf16[64,4096]{1,0:T(8,128)(2,1)S(1)} %get-tuple-element.757), channel_id=1, source_target_pairs={{0,2},{1,3},{2,0},{3,1},{4,6},{5,7},{6,4},{7,5},{8,10},{9,11},{10,... | collective-permute-start | bytes 1572872 | tf_op jit(solution)/shard_map/while/body/eval_jaxpr/ppermute | solution.py:23
  224.6 5.5 %collective-permute-start = (f32[32,1280]{1,0:T(8,128)S(1)}, f32[32,1280]{1,0:T(8,128)S(1)}, u32[]{:S(2)}, u32[]{:S(2)}) collective-permute-start(f32[32,1280]{1,0:T(8,128)S(1)} %broadcast_select_fusion.7), channel_id=1, source_target_pairs={{0,1},{1,0},{2,3},{3,2},{4,5},{5,4},{6,7},{7,6},{8,9},{9,8},{10,11... | collective-permute-start | bytes 491528 | tf_op jit(solution)/shard_map/while/body/eval_jaxpr/ppermute | solution.py:17
  226.6 3.6 collective-permute-start.1
  226.7 19.2 %collective-permute-start.4 = (bf16[64,4096]{1,0:T(8,128)(2,1)S(1)}, bf16[64,4096]{1,0:T(8,128)(2,1)S(1)}, u32[]{:S(2)}, u32[]{:S(2)}) collective-permute-start(bf16[64,4096]{1,0:T(8,128)(2,1)S(1)} %get-tuple-element.663), channel_id=1, source_target_pairs={{0,2},{1,3},{2,0},{3,1},{4,6},{5,7},{6,4},{7,5},{8,10},{9,11},{10,... | collective-permute-start | bytes 1572872 | tf_op jit(solution)/shard_map/while/body/eval_jaxpr/ppermute | solution.py:23
  233.9 4.3 %collective-permute-start.2 = (bf16[32,1024]{1,0:T(8,128)(2,1)S(1)}, bf16[32,1024]{1,0:T(8,128)(2,1)S(1)}, u32[]{:S(2)}, u32[]{:S(2)}) collective-permute-start(bf16[32,1024]{1,0:T(8,128)(2,1)S(1)} %get-tuple-element.756), channel_id=1, source_target_pairs={{0,1},{1,0},{2,3},{3,2},{4,5},{5,4},{6,7},{7,6},{8,9},{9,8},{10,11... | collective-permute-start | bytes 196616 | tf_op jit(solution)/shard_map/while/body/eval_jaxpr/ppermute | solution.py:17
  243.3 9.2 %collective-permute-start.3 = (bf16[64,4096]{1,0:T(8,128)(2,1)S(1)}, bf16[64,4096]{1,0:T(8,128)(2,1)S(1)}, u32[]{:S(2)}, u32[]{:S(2)}) collective-permute-start(bf16[64,4096]{1,0:T(8,128)(2,1)S(1)} %get-tuple-element.757), channel_id=1, source_target_pairs={{0,2},{1,3},{2,0},{3,1},{4,6},{5,7},{6,4},{7,5},{8,10},{9,11},{10,... | collective-permute-start | bytes 1572872 | tf_op jit(solution)/shard_map/while/body/eval_jaxpr/ppermute | solution.py:23
  265.4 5.5 %collective-permute-start = (f32[32,1280]{1,0:T(8,128)S(1)}, f32[32,1280]{1,0:T(8,128)S(1)}, u32[]{:S(2)}, u32[]{:S(2)}) collective-permute-start(f32[32,1280]{1,0:T(8,128)S(1)} %broadcast_select_fusion.7), channel_id=1, source_target_pairs={{0,1},{1,0},{2,3},{3,2},{4,5},{5,4},{6,7},{7,6},{8,9},{9,8},{10,11... | collective-permute-start | bytes 491528 | tf_op jit(solution)/shard_map/while/body/eval_jaxpr/ppermute | solution.py:17
  267.3 3.6 collective-permute-start.1
  267.5 19.2 %collective-permute-start.4 = (bf16[64,4096]{1,0:T(8,128)(2,1)S(1)}, bf16[64,4096]{1,0:T(8,128)(2,1)S(1)}, u32[]{:S(2)}, u32[]{:S(2)}) collective-permute-start(bf16[64,4096]{1,0:T(8,128)(2,1)S(1)} %get-tuple-element.663), channel_id=1, source_target_pairs={{0,2},{1,3},{2,0},{3,1},{4,6},{5,7},{6,4},{7,5},{8,10},{9,11},{10,... | collective-permute-start | bytes 1572872 | tf_op jit(solution)/shard_map/while/body/eval_jaxpr/ppermute | solution.py:23
  274.6 4.3 %collective-permute-start.2 = (bf16[32,1024]{1,0:T(8,128)(2,1)S(1)}, bf16[32,1024]{1,0:T(8,128)(2,1)S(1)}, u32[]{:S(2)}, u32[]{:S(2)}) collective-permute-start(bf16[32,1024]{1,0:T(8,128)(2,1)S(1)} %get-tuple-element.756), channel_id=1, source_target_pairs={{0,1},{1,0},{2,3},{3,2},{4,5},{5,4},{6,7},{7,6},{8,9},{9,8},{10,11... | collective-permute-start | bytes 196616 | tf_op jit(solution)/shard_map/while/body/eval_jaxpr/ppermute | solution.py:17
  284.0 9.2 %collective-permute-start.3 = (bf16[64,4096]{1,0:T(8,128)(2,1)S(1)}, bf16[64,4096]{1,0:T(8,128)(2,1)S(1)}, u32[]{:S(2)}, u32[]{:S(2)}) collective-permute-start(bf16[64,4096]{1,0:T(8,128)(2,1)S(1)} %get-tuple-element.757), channel_id=1, source_target_pairs={{0,2},{1,3},{2,0},{3,1},{4,6},{5,7},{6,4},{7,5},{8,10},{9,11},{10,... | collective-permute-start | bytes 1572872 | tf_op jit(solution)/shard_map/while/body/eval_jaxpr/ppermute | solution.py:23
  306.1 5.5 %collective-permute-start = (f32[32,1280]{1,0:T(8,128)S(1)}, f32[32,1280]{1,0:T(8,128)S(1)}, u32[]{:S(2)}, u32[]{:S(2)}) collective-permute-start(f32[32,1280]{1,0:T(8,128)S(1)} %broadcast_select_fusion.7), channel_id=1, source_target_pairs={{0,1},{1,0},{2,3},{3,2},{4,5},{5,4},{6,7},{7,6},{8,9},{9,8},{10,11... | collective-permute-start | bytes 491528 | tf_op jit(solution)/shard_map/while/body/eval_jaxpr/ppermute | solution.py:17
  308.0 3.6 collective-permute-start.1
  308.2 19.2 %collective-permute-start.4 = (bf16[64,4096]{1,0:T(8,128)(2,1)S(1)}, bf16[64,4096]{1,0:T(8,128)(2,1)S(1)}, u32[]{:S(2)}, u32[]{:S(2)}) collective-permute-start(bf16[64,4096]{1,0:T(8,128)(2,1)S(1)} %get-tuple-element.663), channel_id=1, source_target_pairs={{0,2},{1,3},{2,0},{3,1},{4,6},{5,7},{6,4},{7,5},{8,10},{9,11},{10,... | collective-permute-start | bytes 1572872 | tf_op jit(solution)/shard_map/while/body/eval_jaxpr/ppermute | solution.py:23
  315.4 4.3 %collective-permute-start.2 = (bf16[32,1024]{1,0:T(8,128)(2,1)S(1)}, bf16[32,1024]{1,0:T(8,128)(2,1)S(1)}, u32[]{:S(2)}, u32[]{:S(2)}) collective-permute-start(bf16[32,1024]{1,0:T(8,128)(2,1)S(1)} %get-tuple-element.756), channel_id=1, source_target_pairs={{0,1},{1,0},{2,3},{3,2},{4,5},{5,4},{6,7},{7,6},{8,9},{9,8},{10,11... | collective-permute-start | bytes 196616 | tf_op jit(solution)/shard_map/while/body/eval_jaxpr/ppermute | solution.py:17
  324.7 9.2 %collective-permute-start.3 = (bf16[64,4096]{1,0:T(8,128)(2,1)S(1)}, bf16[64,4096]{1,0:T(8,128)(2,1)S(1)}, u32[]{:S(2)}, u32[]{:S(2)}) collective-permute-start(bf16[64,4096]{1,0:T(8,128)(2,1)S(1)} %get-tuple-element.757), channel_id=1, source_target_pairs={{0,2},{1,3},{2,0},{3,1},{4,6},{5,7},{6,4},{7,5},{8,10},{9,11},{10,... | collective-permute-start | bytes 1572872 | tf_op jit(solution)/shard_map/while/body/eval_jaxpr/ppermute | solution.py:23
  340.6 8.7 %collective-permute-start = (f32[32,1280]{1,0:T(8,128)S(1)}, f32[32,1280]{1,0:T(8,128)S(1)}, u32[]{:S(2)}, u32[]{:S(2)}) collective-permute-start(f32[32,1280]{1,0:T(8,128)S(1)} %broadcast_select_fusion.7), channel_id=1, source_target_pairs={{0,1},{1,0},{2,3},{3,2},{4,5},{5,4},{6,7},{7,6},{8,9},{9,8},{10,11... | collective-permute-start | bytes 491528 | tf_op jit(solution)/shard_map/while/body/eval_jaxpr/ppermute | solution.py:17
  342.5 6.8 %collective-permute-start.1 = (f32[32]{0:T(128)S(1)}, f32[32]{0:T(128)S(1)}, u32[]{:S(2)}, u32[]{:S(2)}) collective-permute-start(f32[32]{0:T(128)S(1)} %broadcast_select_fusion.8), channel_id=1, source_target_pairs={{0,1},{1,0},{2,3},{3,2},{4,5},{5,4},{6,7},{7,6},{8,9},{9,8},{10,11... | collective-permute-start | bytes 392 | tf_op jit(solution)/shard_map/while/body/eval_jaxpr/ppermute | solution.py:17
  342.7 25.3 %collective-permute-start.4 = (bf16[64,4096]{1,0:T(8,128)(2,1)S(1)}, bf16[64,4096]{1,0:T(8,128)(2,1)S(1)}, u32[]{:S(2)}, u32[]{:S(2)}) collective-permute-start(bf16[64,4096]{1,0:T(8,128)(2,1)S(1)} %get-tuple-element.663), channel_id=1, source_target_pairs={{0,2},{1,3},{2,0},{3,1},{4,6},{5,7},{6,4},{7,5},{8,10},{9,11},{10,... | collective-permute-start | bytes 1572872 | tf_op jit(solution)/shard_map/while/body/eval_jaxpr/ppermute | solution.py:23
  349.4 4.3 %collective-permute-start.2 = (bf16[32,1024]{1,0:T(8,128)(2,1)S(1)}, bf16[32,1024]{1,0:T(8,128)(2,1)S(1)}, u32[]{:S(2)}, u32[]{:S(2)}) collective-permute-start(bf16[32,1024]{1,0:T(8,128)(2,1)S(1)} %get-tuple-element.756), channel_id=1, source_target_pairs={{0,1},{1,0},{2,3},{3,2},{4,5},{5,4},{6,7},{7,6},{8,9},{9,8},{10,11... | collective-permute-start | bytes 196616 | tf_op jit(solution)/shard_map/while/body/eval_jaxpr/ppermute | solution.py:17
  353.8 19.4 %collective-permute-start.3 = (bf16[64,4096]{1,0:T(8,128)(2,1)S(1)}, bf16[64,4096]{1,0:T(8,128)(2,1)S(1)}, u32[]{:S(2)}, u32[]{:S(2)}) collective-permute-start(bf16[64,4096]{1,0:T(8,128)(2,1)S(1)} %get-tuple-element.757), channel_id=1, source_target_pairs={{0,2},{1,3},{2,0},{3,1},{4,6},{5,7},{6,4},{7,5},{8,10},{9,11},{10,... | collective-permute-start | bytes 1572872 | tf_op jit(solution)/shard_map/while/body/eval_jaxpr/ppermute | solution.py:23
  379.7 39.3 %copy-start = (bf16[512,4096]{0,1:T(8,128)(2,1)S(1)}, bf16[512,4096]{0,1:T(8,128)(2,1)}, u32[]{:S(2)}) copy-start(bf16[512,4096]{0,1:T(8,128)(2,1)} %copy.8) | copy-start | bytes 12582916
  382.3 36.7 %collective-permute-start.5 = (bf16[512,2048]{0,1:T(8,128)(2,1)S(1)}, bf16[512,2048]{0,1:T(8,128)(2,1)S(1)}, u32[]{:S(2)}, u32[]{:S(2)}) collective-permute-start(bf16[512,2048]{0,1:T(8,128)(2,1)S(1)} %select_bitcast_fusion), channel_id=1, source_target_pairs={{0,2},{1,3},{2,0},{3,1},{4,6},{5,7},{6,4},{7,5},{8,10},{9,11},{10,... | collective-permute-start | bytes 6291464 | tf_op jit(solution)/shard_map/ppermute | solution.py:17
where the time goes:
time: 425 us; the launch traced here: 422 us
  waiting for transfers between devices  143 us (34%)
  matrix products  107 us (25%)
  starting transfers between devices  64.2 us (15%)
  other arithmetic  47.3 us (11%)
  loops' own time  36.2 us (9%)
  local copies, waits for them, and re-layouts  24.1 us (6%)
    ppermute x28, waiting for transfers between devices, partner(): lax.ppermute(value, axis, [(i, i ^ 1 << distance) for i in range(lax.axis...  81.2 us
    ppermute x18, waiting for transfers between devices, shifted(): return lax.ppermute(value, axis, pairs)  62 us
    dot_general x8, matrix products, local_partials(): jnp.dot(scaled, proj_weight, preferred_element_type=jnp.float32)  47.2 us
    dot_general x8, matrix products, local_update(): jnp.dot(collected, out_weight, preferred_element_type=jnp.float32)  40.1 us
    ppermute x28, starting transfers between devices, partner(): lax.ppermute(value, axis, [(i, i ^ 1 << distance) for i in range(lax.axis...  38.2 us
    another operation x1, loops' own time, body(): lax.scan(advance, start, jnp.arange(MICRO + cycle_size - 1, dtype=jnp.int...  35 us
    ppermute x18, starting transfers between devices, shifted(): return lax.ppermute(value, axis, pairs)  26 us
    dynamic_update_slice x9, other arithmetic, advance(): lax.dynamic_update_slice_in_dim(records, jnp.where(leaving[:, None], outg...  18.3 us
  transfers between devices with their start and end apart: 46, of which 27 were waited for; matrix products, arithmetic and copies ran while one was open for 21% of the time, Pallas kernels for 0%

commit v1 on v0

--- a/solution.py
+++ b/solution.py
@@ -1,8 +1,11 @@
+import functools
 import math
 
 import jax
 import jax.numpy as jnp
 from jax import lax
+from jax.experimental import pallas as pl
+from jax.experimental.pallas import tpu as pltpu
 from jax.sharding import PartitionSpec as P
 
 BLOCK = 64
@@ -174,9 +177,356 @@
     return kept
 
 
+MESH = pl.DeviceIdType.MESH
+
+
+def cycle_kernel(
+    sizes,
+    hidden,
+    tokens,
+    cache_hbm,
+    gain,
+    wq_hbm,
+    wo_hbm,
+    out,
+    wq,
+    wo,
+    cache,
+    stage,
+    ready,
+    scaled,
+    partial,
+    squares,
+    psend,
+    precv,
+    att,
+    load_sem,
+    own_sem,
+    st_send,
+    st_recv,
+    p_send,
+    p_recv,
+    a_send,
+    a_recv,
+    out_send,
+    out_recv,
+    keep_sem,
+):
+    shards, head_size, heads = sizes
+    index = lax.axis_index("section")
+    seg = index // shards
+    shard = index % shards
+    across = seg * shards + (1 - shard)
+    along = (1 - seg) * shards + shard
+    width = stage.shape[2]
+    columns = wq.shape[1]
+    query_width = heads * head_size
+    half = MICRO // 2
+    rows = BLOCK // shards
+    span = out.shape[1]
+    context = cache.shape[1]
+    own_rows = pl.ds(pl.multiple_of(shard * rows, rows), rows)
+    other_rows = pl.ds(pl.multiple_of((1 - shard) * rows, rows), rows)
+
+    barrier = pltpu.get_barrier_semaphore()
+    for peer in (across, along):
+        pl.semaphore_signal(barrier, inc=1, device_id={"section": peer}, device_id_type=MESH)
+
+    def own_copy(i):
+        return pltpu.make_async_copy(
+            hidden.at[pl.ds(i * BLOCK, BLOCK)], stage.at[i], own_sem.at[i]
+        )
+
+    load_wq = pltpu.make_async_copy(wq_hbm, wq, load_sem.at[0])
+    load_cache = pltpu.make_async_copy(cache_hbm, cache, load_sem.at[1])
+    load_wo = pltpu.make_async_copy(wo_hbm, wo, load_sem.at[2])
+
+    @pl.when(seg == 0)
+    def _():
+        own_copy(0).start()
+
+    load_wq.start()
+    load_cache.start()
+    load_wo.start()
+
+    def place(i):
+        return jnp.where(i < half, 2 * i, 2 * (i - half) + 1)
+
+    def hidden_copy(i):
+        return pltpu.make_async_remote_copy(
+            src_ref=hidden.at[pl.ds(i * BLOCK, BLOCK)],
+            dst_ref=stage.at[half + i],
+            send_sem=st_send.at[half + i],
+            recv_sem=st_recv.at[half + i],
+            device_id={"section": along},
+            device_id_type=MESH,
+        )
+
+    def state_copy(i):
+        return pltpu.make_async_remote_copy(
+            src_ref=ready.at[i],
+            dst_ref=stage.at[i],
+            send_sem=st_send.at[i],
+            recv_sem=st_recv.at[i],
+            device_id={"section": along},
+            device_id_type=MESH,
+        )
+
+    def partial_copy(i):
+        return pltpu.make_async_remote_copy(
+            src_ref=psend.at[i],
+            dst_ref=precv.at[i],
+            send_sem=p_send.at[i],
+            recv_sem=p_recv.at[i],
+            device_id={"section": across},
+            device_id_type=MESH,
+        )
+
+    def attended_copy(i, sent_rows):
+        return pltpu.make_async_remote_copy(
+            src_ref=att.at[i, sent_rows],
+            dst_ref=att.at[i, sent_rows],
+            send_sem=a_send.at[i],
+            recv_sem=a_recv.at[i],
+            device_id={"section": across},
+            device_id_type=MESH,
+        )
+
+    def out_rows(i):
+        return pl.ds(pl.multiple_of(place(i) * BLOCK, BLOCK), BLOCK)
+
+    def settled_copy(i):
+        return pltpu.make_async_remote_copy(
+            src_ref=ready.at[i, :, pl.ds(0, span)],
+            dst_ref=out.at[out_rows(i)],
+            send_sem=out_send.at[i],
+            recv_sem=out_recv.at[i],
+            device_id={"section": along},
+            device_id_type=MESH,
+        )
+
+    def kept_copy(i):
+        return pltpu.make_async_copy(
+            ready.at[i, :, pl.ds(span, span)], out.at[out_rows(i)], keep_sem.at[i]
+        )
+
+    pl.semaphore_wait(barrier, 2)
+
+    @pl.when(seg == 1)
+    def _():
+        for i in range(half):
+            hidden_copy(i).start()
+
+    @pl.when(seg == 0)
+    def _():
+        for i in range(1, half):
+            own_copy(i).start()
+
+    def project(i):
+        local = (seg == 0) & (i < half)
+
+        @pl.when(local)
+        def _():
+            own_copy(i).wait()
+
+        @pl.when(jnp.logical_not(local))
+        def _():
+            state_copy(i).wait_recv()
+
+        @pl.when(i == 0)
+        def _():
+            load_wq.wait()
+
+        chunk = min(width, 512)
+        total = jnp.zeros((BLOCK, 1), jnp.float32)
+        for start in range(0, width, chunk):
+            cols = pl.ds(start, chunk)
+            piece = stage[i, :, cols].astype(jnp.float32)
+            total = total + jnp.sum(piece * piece, axis=1, keepdims=True)
+            scaled[:, cols] = (piece * gain[:, cols].astype(jnp.float32)).astype(jnp.bfloat16)
+        squares[...] = jnp.broadcast_to(total, squares.shape)
+        step = 512
+        for start in range(0, columns, step):
+            cols = pl.ds(start, min(step, columns - start))
+            partial[:, cols] = jnp.dot(
+                scaled[...], wq[:, cols], preferred_element_type=jnp.float32
+            )
+        psend[i, :, pl.ds(0, columns)] = partial[other_rows, :].astype(jnp.bfloat16)
+        theirs = squares[other_rows, :]
+        coarse = theirs.astype(jnp.bfloat16)
+        fine = (theirs - coarse.astype(jnp.float32)).astype(jnp.bfloat16)
+        psend[i, :, pl.ds(columns, 128)] = coarse
+        psend[i, :, pl.ds(columns + 128, 128)] = fine
+        partial_copy(i).start()
+
+    def attend_rows(i):
+        @pl.when(i == 0)
+        def _():
+            load_cache.wait()
+
+        partial_copy(i).wait_recv()
+        coarse = precv[i, :, pl.ds(columns, 128)].astype(jnp.float32)
+        fine = precv[i, :, pl.ds(columns + 128, 128)].astype(jnp.float32)
+        total_squares = squares[own_rows, :] + coarse + fine
+        factor = lax.rsqrt(total_squares / (width * shards) + EPSILON)[:, :1]
+        fitted = (
+            partial[own_rows, :] + precv[i, :, pl.ds(0, columns)].astype(jnp.float32)
+        ) * factor
+        scale = 1.0 / math.sqrt(head_size)
+        query = jnp.concatenate(
+            [fitted[:, h * head_size : (h + 1) * head_size] for h in range(heads)], axis=0
+        )
+        query = (query * scale).astype(jnp.bfloat16)
+        key_new = fitted[:, query_width : query_width + head_size].astype(jnp.bfloat16)
+        value_new = fitted[:, query_width + head_size :].astype(jnp.bfloat16)
+        key_new = jnp.concatenate([key_new.astype(jnp.float32)] * heads, axis=0)
+        value_new = jnp.concatenate([value_new.astype(jnp.float32)] * heads, axis=0)
+        start = pl.multiple_of(place(i) * rows, rows)
+        held = cache[pl.ds(start, rows)].reshape(rows * context, 2 * head_size)
+        scores = lax.dot_general(
+            query,
+            held[:, :head_size],
+            (((1,), (1,)), ((), ())),
+            preferred_element_type=jnp.float32,
+        )
+        own = jnp.sum(query.astype(jnp.float32) * key_new, axis=1, keepdims=True)
+        limits = tokens[pl.ds(pl.multiple_of(place(i) * BLOCK + shard * rows, rows), rows), :][:, 1:2]
+        row = lax.broadcasted_iota(jnp.int32, (rows, 1), 0) * context
+        low = jnp.concatenate([row] * heads, axis=0)
+        high = jnp.concatenate([row + limits] * heads, axis=0)
+        column = lax.broadcasted_iota(jnp.int32, scores.shape, 1)
+        usable = (column >= low) & (column < high)
+        scores = jnp.where(usable, scores, NEGATIVE)
+        row_top = jnp.maximum(jnp.max(scores, axis=1, keepdims=True), own)
+        raw = jnp.where(usable, jnp.exp(scores - row_top), 0.0)
+        raw_own = jnp.exp(own - row_top)
+        total = jnp.sum(raw, axis=1, keepdims=True) + raw_own
+        weights = (raw / total).astype(jnp.bfloat16)
+        own_weight = (raw_own / total).astype(jnp.bfloat16).astype(jnp.float32)
+        attended = jnp.dot(
+            weights, held[:, head_size:], preferred_element_type=jnp.float32
+        )
+        attended = (attended + own_weight * value_new).astype(jnp.bfloat16)
+        att[i, own_rows, :] = jnp.concatenate(
+            [attended[h * rows : (h + 1) * rows] for h in range(heads)], axis=1
+        )
+        attended_copy(i, own_rows).start()
+
+    def update(i):
+        @pl.when(i == 0)
+        def _():
+            load_wo.wait()
+
+        attended_copy(i, other_rows).wait_recv()
+        depth = tokens[pl.ds(pl.multiple_of(place(i) * BLOCK, BLOCK), BLOCK), :][:, 0:1]
+        active = depth > seg
+        step = min(width, 512)
+        for start in range(0, width, step):
+            cols = pl.ds(start, step)
+            branch = jnp.dot(att[i], wo[:, cols], preferred_element_type=jnp.float32)
+            before = stage[i, :, cols].astype(jnp.float32)
+            ready[i, :, cols] = jnp.where(active, before + branch, before).astype(jnp.bfloat16)
+
+        @pl.when(seg == 0)
+        def _():
+            state_copy(i).start()
+
+        @pl.when(seg == 1)
+        def _():
+            settled_copy(i).start()
+            kept_copy(i).start()
+
+    def step(i, carry):
+        @pl.when(i < MICRO)
+        def _():
+            project(i)
+
+        @pl.when(i > 0)
+        def _():
+            update(i - 1)
+
+        @pl.when(i < MICRO)
+        def _():
+            attend_rows(i)
+
+        return carry
+
+    lax.fori_loop(0, MICRO + 1, step, 0)
+
+    def drain(i, carry):
+        partial_copy(i).wait_send()
+        attended_copy(i, own_rows).wait_send()
+
+        @pl.when(seg == 0)
+        def _():
+            state_copy(i).wait_send()
+            settled_copy(i).wait_recv()
+
+        @pl.when(seg == 1)
+        def _():
+            settled_copy(i).wait_send()
+            kept_copy(i).wait()
+
+        return carry
+
+    lax.fori_loop(0, MICRO, drain, 0)
+
+    @pl.when(seg == 1)
+    def _():
+        for i in range(half):
+            hidden_copy(i).wait_send()
+
+
+def cycle_of_two(hidden, exit_layer, lengths, kv_cache, norm_gain, w_qkv, w_out):
+    shards = 2
+    width = w_qkv.shape[1]
+    columns = w_qkv.shape[2]
+    query_width = w_out.shape[1]
+    head_size = (columns - query_width) // 2
+    heads = query_width // head_size
+    rows = BLOCK // shards
+    tokens = jnp.stack([exit_layer, lengths], axis=1)
+    any_space = pl.BlockSpec(memory_space=pl.ANY)
+    vmem = pl.BlockSpec(memory_space=pltpu.VMEM)
+    dma = pltpu.SemaphoreType.DMA((MICRO,))
+    bf16 = jnp.bfloat16
+    return pl.pallas_call(
+        functools.partial(cycle_kernel, (shards, head_size, heads)),
+        out_shape=jax.ShapeDtypeStruct((MICRO * BLOCK, width // 2), bf16),
+        in_specs=[any_space, vmem, any_space, vmem, any_space, any_space],
+        out_specs=any_space,
+        scratch_shapes=[
+            pltpu.VMEM(w_qkv.shape[1:], bf16),
+            pltpu.VMEM(w_out.shape[1:], bf16),
+            pltpu.VMEM(kv_cache.shape[1:], bf16),
+            pltpu.VMEM((MICRO, BLOCK, width), bf16),
+            pltpu.VMEM((MICRO, BLOCK, width), bf16),
+            pltpu.VMEM((BLOCK, width), bf16),
+            pltpu.VMEM((BLOCK, columns), jnp.float32),
+            pltpu.VMEM((BLOCK, 128), jnp.float32),
+            pltpu.VMEM((MICRO, rows, columns + 256), bf16),
+            pltpu.VMEM((MICRO, rows, columns + 256), bf16),
+            pltpu.VMEM((MICRO, BLOCK, query_width), bf16),
+            pltpu.SemaphoreType.DMA((3,)),
+        ]
+        + [dma] * 10,
+        compiler_params=pltpu.CompilerParams(
+            collective_id=0, has_side_effects=True, vmem_limit_bytes=60 << 20
+        ),
+        name="cycle",
+    )(hidden[0], tokens, kv_cache[0], norm_gain, w_qkv[0], w_out[0])
+
+
+def chosen(devices, *arguments):
+    shards = max(2, devices // 4)
+    if shards == 2 and devices // shards == 2:
+        return cycle_of_two(*arguments)
+    return body(*arguments)
+
+
 def solution(mesh):
     return jax.shard_map(
-        body,
+        functools.partial(chosen, mesh.shape["section"]),
         mesh=mesh,
         in_specs=(
             P("section", "blk", None),

time: 425 us -> 131 us (0.31)
  waiting for transfers between devices: 143 us -> 0 us
  Pallas kernels: 0 us -> 126 us
  matrix products: 107 us -> 0 us
  starting transfers between devices: 64.2 us -> 0 us
  other arithmetic: 47.3 us -> 0.71 us
  loops' own time: 36.2 us -> 0 us
  local copies, waits for them, and re-layouts: 24.1 us -> 4.02 us
    ppermute x46 -> x0, waiting for transfers between devices: 143 us -> none  [the longest x28 81.2 us: partner(): lax.ppermute(value, axis, [(i, i ^ 1 << distance) for i in range(lax.axis...]
    pallas_call x0 -> x1, Pallas kernels: none -> 126 us  [cycle_of_two(): pl.pallas_call(functools.partial(cycle_kernel, (shards, head_size, heads)...]
    dot_general x40 -> x0, matrix products: 107 us -> none  [the longest x8 47.2 us: local_partials(): jnp.dot(scaled, proj_weight, preferred_element_type=jnp.float32)]
    ppermute x46 -> x0, starting transfers between devices: 64.2 us -> none  [the longest x28 38.2 us: partner(): lax.ppermute(value, axis, [(i, i ^ 1 << distance) for i in range(lax.axis...]
    another operation x28 -> x0, loops' own time: 36.2 us -> none  [the longest x1 35 us: body(): lax.scan(advance, start, jnp.arange(MICRO + cycle_size - 1, dtype=jnp.int...]
    dynamic_update_slice x9 -> x0, other arithmetic: 18.3 us -> none  [advance(): lax.dynamic_update_slice_in_dim(records, jnp.where(leaving[:, None], outg...]
    select_n x28 -> x0, other arithmetic: 14.5 us -> none  [the longest x9 11.7 us: advance(): relayed = jnp.where(on_turn & (segment_index > 0), own_block, arriving)]
    dynamic_slice x17 -> x0, local copies, waits for them, and re-layouts: 11.4 us -> none  [the longest x8 6.07 us: advance(): lax.dynamic_slice_in_dim(lengths, slot * BLOCK + shard_index * group_rows...]
  transfers between devices with their start and end apart: 46 -> 0, of which waited for: 27 -> 0; matrix products, arithmetic and copies ran while one was open for 21% -> 0% of each run, Pallas kernels for 0% -> 0%
where the time goes in v1:
time: 131 us
  Pallas kernels  126 us (96%)
  local copies, waits for them, and re-layouts  4.02 us (3%)
    pallas_call x1, Pallas kernels, cycle_of_two(): pl.pallas_call(functools.partial(cycle_kernel, (shards, head_size, heads)...  126 us
    unnamed x1, local copies, waits for them, and re-layouts  3.16 us

profile of v1, /device:TPU:0, one launch (start us, length us, event | category | flops | bytes accessed | tf_op | source)
XLA Modules:
  0.0 130.6 jit_solution(12497164742988918980)
XLA Ops:
  0.0 0.7 pad_add_fusion
  0.7 0.9 copy.10.tokens
  1.6 125.9 %cycle.1 = bf16[512,2048]{1,0:T(8,128)(2,1)} custom-call(bf16[256,4096]{1,0:T(8,128)(2,1)} %bitcast.8, s32[512,2]{1,0:T(8,128)} %copy.10.tokens, bf16[256,16,256]{2,1,0:T(8,128)(2,1)} %bitcast.9, bf16[1,4096]{1,0:T(2,128)(2,1)} %gain.1, bf16[4096,1280]{1,0:T(8,128)(2,1)} %bitcast.6, bf16[1024,4096]{1,0:T(8,128)(2,1)} %bitcast.7), custom_call_target="tpu_custom_call" | custom-call | tf_op jit(solution)/shard_map/cycle/pallas_call | solution.py:493
  127.4 3.2 %copy.12 = bf16[512,2048]{1,0:T(8,128)(2,1)} copy(bf16[512,2048]{1,0:T(8,128)(2,1)} %cycle.1) | data formatting | bytes 4194304

commit v2 on v1

--- a/solution.py
+++ b/solution.py
@@ -200,10 +200,22 @@
     psend,
     precv,
     att,
+    wx,
+    att_in,
     load_sem,
+    wy_send,
+    wy_recv,
+    wz_send,
+    wz_recv,
+    wd_send,
+    wd_recv,
     own_sem,
-    st_send,
-    st_recv,
+    h_send,
+    h_recv,
+    lo_send,
+    lo_recv,
+    hi_send,
+    hi_recv,
     p_send,
     p_recv,
     a_send,
@@ -228,15 +240,74 @@
     own_rows = pl.ds(pl.multiple_of(shard * rows, rows), rows)
     other_rows = pl.ds(pl.multiple_of((1 - shard) * rows, rows), rows)
 
+    place_blk = lax.axis_index("blk")
+    chips = wz_send.shape[0] + 1
+    chip = place_blk // 2
+    core = place_blk % 2
+    piece = wx.shape[0] // (2 * chips)
+
+    def on_chip(steps):
+        return (chip + steps + chips) % chips
+
     barrier = pltpu.get_barrier_semaphore()
     for peer in (across, along):
         pl.semaphore_signal(barrier, inc=1, device_id={"section": peer}, device_id_type=MESH)
+    for steps in range(1, chips):
+        pl.semaphore_signal(
+            barrier,
+            inc=1,
+            device_id={"blk": on_chip(steps) * 2 + core},
+            device_id_type=MESH,
+        )
+    pl.semaphore_signal(
+        barrier, inc=1, device_id={"blk": chip * 2 + 1 - core}, device_id_type=MESH
+    )
+
+    def piece_rows(owner):
+        return pl.ds(pl.multiple_of(owner * piece, piece), piece)
+
+    def weight_along():
+        return pltpu.make_async_remote_copy(
+            src_ref=wo_hbm.at[piece_rows(place_blk), pl.ds(span, span)],
+            dst_ref=wx.at[piece_rows(place_blk)],
+            send_sem=wy_send.at[0],
+            recv_sem=wy_recv.at[0],
+            device_id={"section": along},
+            device_id_type=MESH,
+        )
+
+    def weight_chips(steps, owner):
+        return pltpu.make_async_remote_copy(
+            src_ref=wx.at[piece_rows(owner)],
+            dst_ref=wx.at[piece_rows(owner)],
+            send_sem=wz_send.at[steps - 1],
+            recv_sem=wz_recv.at[steps - 1],
+            device_id={"blk": on_chip(steps) * 2 + core},
+            device_id_type=MESH,
+        )
+
+    def weight_cores(steps, owner):
+        return pltpu.make_async_remote_copy(
+            src_ref=wx.at[piece_rows(owner)],
+            dst_ref=wx.at[piece_rows(owner)],
+            send_sem=wd_send.at[steps],
+            recv_sem=wd_recv.at[steps],
+            device_id={"blk": chip * 2 + 1 - core},
+            device_id_type=MESH,
+        )
 
     def own_copy(i):
         return pltpu.make_async_copy(
             hidden.at[pl.ds(i * BLOCK, BLOCK)], stage.at[i], own_sem.at[i]
         )
 
+    def rest_copy(i):
+        return pltpu.make_async_copy(
+            hidden.at[pl.ds(i * BLOCK, BLOCK), pl.ds(span, span)],
+            stage.at[half + i, :, pl.ds(span, span)],
+            own_sem.at[i],
+        )
+
     load_wq = pltpu.make_async_copy(wq_hbm, wq, load_sem.at[0])
     load_cache = pltpu.make_async_copy(cache_hbm, cache, load_sem.at[1])
     load_wo = pltpu.make_async_copy(wo_hbm, wo, load_sem.at[2])
@@ -247,7 +318,6 @@
 
     load_wq.start()
     load_cache.start()
-    load_wo.start()
 
     def place(i):
         return jnp.where(i < half, 2 * i, 2 * (i - half) + 1)
@@ -256,18 +326,38 @@
         return pltpu.make_async_remote_copy(
             src_ref=hidden.at[pl.ds(i * BLOCK, BLOCK)],
             dst_ref=stage.at[half + i],
-            send_sem=st_send.at[half + i],
-            recv_sem=st_recv.at[half + i],
+            send_sem=h_send.at[i],
+            recv_sem=h_recv.at[i],
             device_id={"section": along},
             device_id_type=MESH,
         )
 
-    def state_copy(i):
-        return pltpu.make_async_remote_copy(
-            src_ref=ready.at[i],
-            dst_ref=stage.at[i],
-            send_sem=st_send.at[i],
-            recv_sem=st_recv.at[i],
+    def low_copy(i):
+        return pltpu.make_async_remote_copy(
+            src_ref=ready.at[i, :, pl.ds(0, span)],
+            dst_ref=stage.at[i, :, pl.ds(0, span)],
+            send_sem=lo_send.at[i],
+            recv_sem=lo_recv.at[i],
+            device_id={"section": along},
+            device_id_type=MESH,
+        )
+
+    def high_copy(i):
+        return pltpu.make_async_remote_copy(
+            src_ref=ready.at[i, :, pl.ds(span, span)],
+            dst_ref=stage.at[i, :, pl.ds(span, span)],
+            send_sem=hi_send.at[i],
+            recv_sem=hi_recv.at[i],
+            device_id={"section": along},
+            device_id_type=MESH,
+        )
+
+    def branch_copy(i):
+        return pltpu.make_async_remote_copy(
+            src_ref=att.at[i],
+            dst_ref=att_in.at[i - half],
+            send_sem=hi_send.at[i],
+            recv_sem=hi_recv.at[i],
             device_id={"section": along},
             device_id_type=MESH,
         )
@@ -310,17 +400,24 @@
             ready.at[i, :, pl.ds(span, span)], out.at[out_rows(i)], keep_sem.at[i]
         )
 
-    pl.semaphore_wait(barrier, 2)
+    pl.semaphore_wait(barrier, chips + 2)
+
+    @pl.when(seg == 0)
+    def _():
+        weight_along().start()
+        for i in range(1, half):
+            own_copy(i).start()
 
     @pl.when(seg == 1)
     def _():
         for i in range(half):
             hidden_copy(i).start()
-
-    @pl.when(seg == 0)
-    def _():
-        for i in range(1, half):
-            own_copy(i).start()
+        for i in range(half):
+            rest_copy(i).start()
+        weight_along().wait_recv()
+        for steps in range(1, chips):
+            weight_chips(steps, place_blk).start()
+        weight_cores(0, place_blk).start()
 
     def project(i):
         local = (seg == 0) & (i < half)
@@ -329,13 +426,52 @@
         def _():
             own_copy(i).wait()
 
-        @pl.when(jnp.logical_not(local))
-        def _():
-            state_copy(i).wait_recv()
+        @pl.when((seg == 0) & (i >= half))
+        def _():
+            hidden_copy(i - half).wait_recv()
+
+        @pl.when((seg == 1) & (i == half - 1))
+        def _():
+            for steps in range(1, chips):
+                owner = on_chip(-steps) * 2 + core
+                weight_chips(steps, owner).wait_recv()
+                weight_cores(steps, owner).start()
+
+        @pl.when((seg == 1) & (i < half))
+        def _():
+            high_copy(i).wait_recv()
+
+        @pl.when((seg == 1) & (i == half))
+        def _():
+            for steps in range(chips):
+                weight_cores(steps, on_chip(-steps) * 2 + 1 - core).wait_recv()
+
+        @pl.when((seg == 1) & (i >= half))
+        def _():
+            rest_copy(i - half).wait()
+            branch_copy(i).wait_recv()
+            depth = tokens[pl.ds(pl.multiple_of(place(i) * BLOCK, BLOCK), BLOCK), :][:, 0:1]
+            size = min(span, 512)
+            for start in range(0, span, size):
+                branch = jnp.dot(
+                    att_in[i - half],
+                    wx[:, pl.ds(start, size)],
+                    preferred_element_type=jnp.float32,
+                )
+                cols = pl.ds(span + start, size)
+                before = stage[i, :, cols].astype(jnp.float32)
+                stage[i, :, cols] = jnp.where(depth > 0, before + branch, before).astype(
+                    jnp.bfloat16
+                )
+
+        @pl.when(seg == 1)
+        def _():
+            low_copy(i).wait_recv()
 
         @pl.when(i == 0)
         def _():
             load_wq.wait()
+            load_wo.start()
 
         chunk = min(width, 512)
         total = jnp.zeros((BLOCK, 1), jnp.float32)
@@ -420,20 +556,40 @@
         attended_copy(i, other_rows).wait_recv()
         depth = tokens[pl.ds(pl.multiple_of(place(i) * BLOCK, BLOCK), BLOCK), :][:, 0:1]
         active = depth > seg
-        step = min(width, 512)
-        for start in range(0, width, step):
-            cols = pl.ds(start, step)
-            branch = jnp.dot(att[i], wo[:, cols], preferred_element_type=jnp.float32)
-            before = stage[i, :, cols].astype(jnp.float32)
-            ready[i, :, cols] = jnp.where(active, before + branch, before).astype(jnp.bfloat16)
+        step = min(span, 512)
+        brief = (seg == 0) & (i >= half)
+
+        def fill(first):
+            for start in range(first, first + span, step):
+                cols = pl.ds(start, step)
+                branch = jnp.dot(att[i], wo[:, cols], preferred_element_type=jnp.float32)
+                before = stage[i, :, cols].astype(jnp.float32)
+                ready[i, :, cols] = jnp.where(active, before + branch, before).astype(jnp.bfloat16)
+
+        @pl.when(brief)
+        def _():
+            branch_copy(i).start()
+
+        fill(0)
 
         @pl.when(seg == 0)
         def _():
-            state_copy(i).start()
+            low_copy(i).start()
 
         @pl.when(seg == 1)
         def _():
             settled_copy(i).start()
+
+        @pl.when(jnp.logical_not(brief))
+        def _():
+            fill(span)
+
+        @pl.when((seg == 0) & (i < half))
+        def _():
+            high_copy(i).start()
+
+        @pl.when(seg == 1)
+        def _():
             kept_copy(i).start()
 
     def step(i, carry):
@@ -459,7 +615,7 @@
 
         @pl.when(seg == 0)
         def _():
-            state_copy(i).wait_send()
+            low_copy(i).wait_send()
             settled_copy(i).wait_recv()
 
         @pl.when(seg == 1)
@@ -470,14 +626,25 @@
         return carry
 
     lax.fori_loop(0, MICRO, drain, 0)
+
+    @pl.when(seg == 0)
+    def _():
+        weight_along().wait_send()
+        for i in range(half):
+            high_copy(i).wait_send()
+            branch_copy(half + i).wait_send()
 
     @pl.when(seg == 1)
     def _():
         for i in range(half):
             hidden_copy(i).wait_send()
-
-
-def cycle_of_two(hidden, exit_layer, lengths, kv_cache, norm_gain, w_qkv, w_out):
+        for steps in range(1, chips):
+            weight_chips(steps, place_blk).wait_send()
+        for steps in range(chips):
+            weight_cores(steps, on_chip(-steps) * 2 + core).wait_send()
+
+
+def cycle_of_two(chips, hidden, exit_layer, lengths, kv_cache, norm_gain, w_qkv, w_out):
     shards = 2
     width = w_qkv.shape[1]
     columns = w_qkv.shape[2]
@@ -507,9 +674,17 @@
             pltpu.VMEM((MICRO, rows, columns + 256), bf16),
             pltpu.VMEM((MICRO, rows, columns + 256), bf16),
             pltpu.VMEM((MICRO, BLOCK, query_width), bf16),
+            pltpu.VMEM((query_width, width // 2), bf16),
+            pltpu.VMEM((MICRO // 2, BLOCK, query_width), bf16),
             pltpu.SemaphoreType.DMA((3,)),
+            pltpu.SemaphoreType.DMA((1,)),
+            pltpu.SemaphoreType.DMA((1,)),
+            pltpu.SemaphoreType.DMA((chips - 1,)),
+            pltpu.SemaphoreType.DMA((chips - 1,)),
+            pltpu.SemaphoreType.DMA((chips,)),
+            pltpu.SemaphoreType.DMA((chips,)),
         ]
-        + [dma] * 10,
+        + [dma] * 14,
         compiler_params=pltpu.CompilerParams(
             collective_id=0, has_side_effects=True, vmem_limit_bytes=60 << 20
         ),
@@ -517,16 +692,16 @@
     )(hidden[0], tokens, kv_cache[0], norm_gain, w_qkv[0], w_out[0])
 
 
-def chosen(devices, *arguments):
+def chosen(batches, devices, *arguments):
     shards = max(2, devices // 4)
     if shards == 2 and devices // shards == 2:
-        return cycle_of_two(*arguments)
+        return cycle_of_two(batches // 2, *arguments)
     return body(*arguments)
 
 
 def solution(mesh):
     return jax.shard_map(
-        functools.partial(chosen, mesh.shape["section"]),
+        functools.partial(chosen, mesh.shape["blk"], mesh.shape["section"]),
         mesh=mesh,
         in_specs=(
             P("section", "blk", None),

time: 131 us -> 120 us (0.916)
  Pallas kernels: 126 us -> 115 us
    pallas_call x1, Pallas kernels: 126 us -> 115 us  [cycle_of_two(): pl.pallas_call(functools.partial(cycle_kernel, (shards, head_size, heads)...]
where the time goes in v2:
time: 120 us
  Pallas kernels  115 us (96%)
  local copies, waits for them, and re-layouts  4.02 us (3%)
    pallas_call x1, Pallas kernels, cycle_of_two(): pl.pallas_call(functools.partial(cycle_kernel, (shards, head_size, heads)...  115 us
    unnamed x1, local copies, waits for them, and re-layouts  3.16 us

profile of v2, /device:TPU:0, one launch (start us, length us, event | category | flops | bytes accessed | tf_op | source)
XLA Modules:
  0.0 119.6 jit_solution(11511856160158596222)
XLA Ops:
  0.0 0.7 pad_add_fusion
  0.7 0.9 copy.10.tokens
  1.6 114.9 %cycle.1 = bf16[512,2048]{1,0:T(8,128)(2,1)} custom-call(bf16[256,4096]{1,0:T(8,128)(2,1)} %bitcast.8, s32[512,2]{1,0:T(8,128)} %copy.10.tokens, bf16[256,16,256]{2,1,0:T(8,128)(2,1)} %bitcast.9, bf16[1,4096]{1,0:T(2,128)(2,1)} %gain.1, bf16[4096,1280]{1,0:T(8,128)(2,1)} %bitcast.6, bf16[1024,4096]{1,0:T(8,128)(2,1)} %bitcast.7), custom_call_target="tpu_custom_call" | custom-call | tf_op jit(solution)/shard_map/cycle/pallas_call | solution.py:660
  116.5 3.2 %copy.12 = bf16[512,2048]{1,0:T(8,128)(2,1)} copy(bf16[512,2048]{1,0:T(8,128)(2,1)} %cycle.1) | data formatting | bytes 4194304

commit v3 on v2

--- a/solution.py
+++ b/solution.py
@@ -220,8 +220,10 @@
     p_recv,
     a_send,
     a_recv,
-    out_send,
-    out_recv,
+    r_send,
+    r_recv,
+    d_send,
+    d_recv,
     keep_sem,
 ):
     shards, head_size, heads = sizes
@@ -230,6 +232,7 @@
     shard = index % shards
     across = seg * shards + (1 - shard)
     along = (1 - seg) * shards + shard
+    corner = (1 - seg) * shards + (1 - shard)
     width = stage.shape[2]
     columns = wq.shape[1]
     query_width = heads * head_size
@@ -250,7 +253,7 @@
         return (chip + steps + chips) % chips
 
     barrier = pltpu.get_barrier_semaphore()
-    for peer in (across, along):
+    for peer in (across, along, corner):
         pl.semaphore_signal(barrier, inc=1, device_id={"section": peer}, device_id_type=MESH)
     for steps in range(1, chips):
         pl.semaphore_signal(
@@ -268,7 +271,9 @@
 
     def weight_along():
         return pltpu.make_async_remote_copy(
-            src_ref=wo_hbm.at[piece_rows(place_blk), pl.ds(span, span)],
+            src_ref=wo_hbm.at[
+                piece_rows(place_blk), pl.ds(pl.multiple_of((1 - seg) * span, 128), span)
+            ],
             dst_ref=wx.at[piece_rows(place_blk)],
             send_sem=wy_send.at[0],
             recv_sem=wy_recv.at[0],
@@ -352,13 +357,23 @@
             device_id_type=MESH,
         )
 
-    def branch_copy(i):
-        return pltpu.make_async_remote_copy(
-            src_ref=att.at[i],
-            dst_ref=att_in.at[i - half],
-            send_sem=hi_send.at[i],
-            recv_sem=hi_recv.at[i],
+    def branch_copy(i, sent_rows):
+        return pltpu.make_async_remote_copy(
+            src_ref=att.at[i, sent_rows],
+            dst_ref=att_in.at[i, sent_rows],
+            send_sem=r_send.at[i],
+            recv_sem=r_recv.at[i],
             device_id={"section": along},
+            device_id_type=MESH,
+        )
+
+    def corner_copy(i, sent_rows):
+        return pltpu.make_async_remote_copy(
+            src_ref=att.at[i, sent_rows],
+            dst_ref=att_in.at[i, sent_rows],
+            send_sem=d_send.at[i],
+            recv_sem=d_recv.at[i],
+            device_id={"section": corner},
             device_id_type=MESH,
         )
 
@@ -385,22 +400,33 @@
     def out_rows(i):
         return pl.ds(pl.multiple_of(place(i) * BLOCK, BLOCK), BLOCK)
 
-    def settled_copy(i):
-        return pltpu.make_async_remote_copy(
-            src_ref=ready.at[i, :, pl.ds(0, span)],
-            dst_ref=out.at[out_rows(i)],
-            send_sem=out_send.at[i],
-            recv_sem=out_recv.at[i],
-            device_id={"section": along},
-            device_id_type=MESH,
-        )
-
     def kept_copy(i):
         return pltpu.make_async_copy(
             ready.at[i, :, pl.ds(span, span)], out.at[out_rows(i)], keep_sem.at[i]
         )
 
-    pl.semaphore_wait(barrier, chips + 2)
+    def final_copy(i):
+        return pltpu.make_async_copy(
+            stage.at[i, :, pl.ds(0, span)], out.at[out_rows(i)], keep_sem.at[i]
+        )
+
+    def spread():
+        weight_along().wait_recv()
+        for steps in range(1, chips):
+            weight_chips(steps, place_blk).start()
+        weight_cores(0, place_blk).start()
+
+    def pass_on():
+        for steps in range(1, chips):
+            owner = on_chip(-steps) * 2 + core
+            weight_chips(steps, owner).wait_recv()
+            weight_cores(steps, owner).start()
+
+    def gathered():
+        for steps in range(chips):
+            weight_cores(steps, on_chip(-steps) * 2 + 1 - core).wait_recv()
+
+    pl.semaphore_wait(barrier, chips + 3)
 
     @pl.when(seg == 0)
     def _():
@@ -410,14 +436,13 @@
 
     @pl.when(seg == 1)
     def _():
-        for i in range(half):
+        hidden_copy(0).start()
+        weight_along().start()
+        for i in range(1, half):
             hidden_copy(i).start()
         for i in range(half):
             rest_copy(i).start()
-        weight_along().wait_recv()
-        for steps in range(1, chips):
-            weight_chips(steps, place_blk).start()
-        weight_cores(0, place_blk).start()
+        spread()
 
     def project(i):
         local = (seg == 0) & (i < half)
@@ -426,16 +451,17 @@
         def _():
             own_copy(i).wait()
 
+        @pl.when((seg == 0) & (i == half))
+        def _():
+            spread()
+
         @pl.when((seg == 0) & (i >= half))
         def _():
             hidden_copy(i - half).wait_recv()
 
         @pl.when((seg == 1) & (i == half - 1))
         def _():
-            for steps in range(1, chips):
-                owner = on_chip(-steps) * 2 + core
-                weight_chips(steps, owner).wait_recv()
-                weight_cores(steps, owner).start()
+            pass_on()
 
         @pl.when((seg == 1) & (i < half))
         def _():
@@ -443,18 +469,18 @@
 
         @pl.when((seg == 1) & (i == half))
         def _():
-            for steps in range(chips):
-                weight_cores(steps, on_chip(-steps) * 2 + 1 - core).wait_recv()
+            gathered()
 
         @pl.when((seg == 1) & (i >= half))
         def _():
             rest_copy(i - half).wait()
-            branch_copy(i).wait_recv()
+            branch_copy(i, own_rows).wait_recv()
+            corner_copy(i, other_rows).wait_recv()
             depth = tokens[pl.ds(pl.multiple_of(place(i) * BLOCK, BLOCK), BLOCK), :][:, 0:1]
             size = min(span, 512)
             for start in range(0, span, size):
                 branch = jnp.dot(
-                    att_in[i - half],
+                    att_in[i],
                     wx[:, pl.ds(start, size)],
                     preferred_element_type=jnp.float32,
                 )
@@ -548,6 +574,11 @@
         )
         attended_copy(i, own_rows).start()
 
+        @pl.when((seg == 1) | (i >= half))
+        def _():
+            corner_copy(i, own_rows).start()
+            branch_copy(i, own_rows).start()
+
     def update(i):
         @pl.when(i == 0)
         def _():
@@ -557,7 +588,6 @@
         depth = tokens[pl.ds(pl.multiple_of(place(i) * BLOCK, BLOCK), BLOCK), :][:, 0:1]
         active = depth > seg
         step = min(span, 512)
-        brief = (seg == 0) & (i >= half)
 
         def fill(first):
             for start in range(first, first + span, step):
@@ -566,21 +596,12 @@
                 before = stage[i, :, cols].astype(jnp.float32)
                 ready[i, :, cols] = jnp.where(active, before + branch, before).astype(jnp.bfloat16)
 
-        @pl.when(brief)
-        def _():
-            branch_copy(i).start()
-
-        fill(0)
-
         @pl.when(seg == 0)
         def _():
+            fill(0)
             low_copy(i).start()
 
-        @pl.when(seg == 1)
-        def _():
-            settled_copy(i).start()
-
-        @pl.when(jnp.logical_not(brief))
+        @pl.when((seg == 1) | (i < half))
         def _():
             fill(span)
 
@@ -608,6 +629,25 @@
         return carry
 
     lax.fori_loop(0, MICRO + 1, step, 0)
+
+    def finish(i, carry):
+        branch_copy(i, own_rows).wait_recv()
+        corner_copy(i, other_rows).wait_recv()
+        depth = tokens[pl.ds(pl.multiple_of(place(i) * BLOCK, BLOCK), BLOCK), :][:, 0:1]
+        size = min(span, 512)
+        for start in range(0, span, size):
+            cols = pl.ds(start, size)
+            branch = jnp.dot(att_in[i], wx[:, cols], preferred_element_type=jnp.float32)
+            before = ready[i, :, cols].astype(jnp.float32)
+            stage[i, :, cols] = jnp.where(depth > 1, before + branch, before).astype(jnp.bfloat16)
+        final_copy(i).start()
+        return carry
+
+    @pl.when(seg == 0)
+    def _():
+        pass_on()
+        gathered()
+        lax.fori_loop(0, MICRO, finish, 0)
 
     def drain(i, carry):
         partial_copy(i).wait_send()
@@ -616,32 +656,36 @@
         @pl.when(seg == 0)
         def _():
             low_copy(i).wait_send()
-            settled_copy(i).wait_recv()
+            final_copy(i).wait()
 
         @pl.when(seg == 1)
         def _():
-            settled_copy(i).wait_send()
             kept_copy(i).wait()
 
+        @pl.when((seg == 1) | (i >= half))
+        def _():
+            branch_copy(i, own_rows).wait_send()
+            corner_copy(i, own_rows).wait_send()
+
         return carry
 
     lax.fori_loop(0, MICRO, drain, 0)
+
+    weight_along().wait_send()
+    for steps in range(1, chips):
+        weight_chips(steps, place_blk).wait_send()
+    for steps in range(chips):
+        weight_cores(steps, on_chip(-steps) * 2 + core).wait_send()
 
     @pl.when(seg == 0)
     def _():
-        weight_along().wait_send()
         for i in range(half):
             high_copy(i).wait_send()
-            branch_copy(half + i).wait_send()
 
     @pl.when(seg == 1)
     def _():
         for i in range(half):
             hidden_copy(i).wait_send()
-        for steps in range(1, chips):
-            weight_chips(steps, place_blk).wait_send()
-        for steps in range(chips):
-            weight_cores(steps, on_chip(-steps) * 2 + core).wait_send()
 
 
 def cycle_of_two(chips, hidden, exit_layer, lengths, kv_cache, norm_gain, w_qkv, w_out):
@@ -675,7 +719,7 @@
             pltpu.VMEM((MICRO, rows, columns + 256), bf16),
             pltpu.VMEM((MICRO, BLOCK, query_width), bf16),
             pltpu.VMEM((query_width, width // 2), bf16),
-            pltpu.VMEM((MICRO // 2, BLOCK, query_width), bf16),
+            pltpu.VMEM((MICRO, BLOCK, query_width), bf16),
             pltpu.SemaphoreType.DMA((3,)),
             pltpu.SemaphoreType.DMA((1,)),
             pltpu.SemaphoreType.DMA((1,)),
@@ -684,7 +728,7 @@
             pltpu.SemaphoreType.DMA((chips,)),
             pltpu.SemaphoreType.DMA((chips,)),
         ]
-        + [dma] * 14,
+        + [dma] * 16,
         compiler_params=pltpu.CompilerParams(
             collective_id=0, has_side_effects=True, vmem_limit_bytes=60 << 20
         ),

time: 120 us -> 120 us (level)
  no operation moved by 1% of the time
where the time goes in v3:
time: 120 us; the launch traced here: 119 us
  Pallas kernels  115 us (96%)
  local copies, waits for them, and re-layouts  4.02 us (3%)
    pallas_call x1, Pallas kernels, cycle_of_two(): pl.pallas_call(functools.partial(cycle_kernel, (shards, head_size, heads)...  115 us
    unnamed x1, local copies, waits for them, and re-layouts  3.16 us

profile of v3, /device:TPU:0, one launch (start us, length us, event | category | flops | bytes accessed | tf_op | source)
XLA Modules:
  0.0 119.4 jit_solution(4287008868200046789)
XLA Ops:
  0.0 0.7 pad_add_fusion
  0.7 0.9 copy.10.tokens
  1.6 114.6 %cycle.1 = bf16[512,2048]{1,0:T(8,128)(2,1)} custom-call(bf16[256,4096]{1,0:T(8,128)(2,1)} %bitcast.8, s32[512,2]{1,0:T(8,128)} %copy.10.tokens, bf16[256,16,256]{2,1,0:T(8,128)(2,1)} %bitcast.9, bf16[1,4096]{1,0:T(2,128)(2,1)} %gain.1, bf16[4096,1280]{1,0:T(8,128)(2,1)} %bitcast.6, bf16[1024,4096]{1,0:T(8,128)(2,1)} %bitcast.7), custom_call_target="tpu_custom_call" | custom-call | tf_op jit(solution)/shard_map/cycle/pallas_call | solution.py:704
  116.2 3.2 %copy.12 = bf16[512,2048]{1,0:T(8,128)(2,1)} copy(bf16[512,2048]{1,0:T(8,128)(2,1)} %cycle.1) | data formatting | bytes 4194304
